TPU v7x, 256 devices: a whole 4x4x8 slice. The times are simulated.
256 devices in a mesh: grp: 32 (over z, x), tp: 8 (over y, core).
Axes of the slice: x: 4, y: 4, z: 8, core: 2. Of those that a mesh axis runs over, the one named last changes fastest.
Arguments:
- suffix_cache: bfloat16 [128, 512, 2, 1024], P('grp', None, None, 'tp'), may hold values from -6 to 6
- prompt_cache: bfloat16 [64, 512, 2, 1024], P('grp', None, None, 'tp'), may hold values from -6 to 6
- query_first: bfloat16 [128, 8192], P('grp', 'tp'), may hold values from -45 to 45
- fresh_first: bfloat16 [128, 2, 1024], P('grp', None, 'tp'), may hold values from -6 to 6
- query_second: bfloat16 [128, 8192], P('grp', 'tp'), may hold values from -45 to 45
- fresh_second: bfloat16 [128, 2, 1024], P('grp', None, 'tp'), may hold values from -6 to 6
- out_weight: bfloat16 [8192, 4096], P('tp'), may hold values from -1 to 1
- suffix_len: int32 [128], replicated, may hold values from 0 to 511, as said below
- prompt_slot: int32 [128], P('grp'), may hold values from -1 to 1, as said below
- moves: int32 [8, 5], replicated, may hold values from 0 to 31, as said below
Outputs:
- out_first: bfloat16 [128, 4096], P('grp', 'tp')
- out_second: bfloat16 [128, 4096], P('grp', 'tp')
Inputs may be any that keep to these rules, and one draw needn't show every extreme that they name: `suffix_len`: 0 exactly on empty slots, 1 or more on live ones. Every group has exactly one empty slot before the migration. The source of every move is live and its length is 384 or more; some source has 511. `prompt_slot`: each group's live samples read its prompt slots; in every destination group all live samples read one prompt slot and the other is free. `moves`: source groups are distinct, destination groups are distinct, and no group is both. The destination slot is the destination group's empty slot and the destination prompt slot is its free prompt slot.
All inputs are finite; a program needn't handle non-finite values.
Results may differ from a plain program's by a relative error of at most 0.0058.
Values may be sent and summed in bfloat16 or wider, within the bound.
No kernel may reach another device: no remote copies, remote signals or barrier semaphores. Data moves between devices by JAX's collectives and lax.ppermute only.
A program may use at most 128 MiB of HBM per device.

v0:
```python
import jax
import jax.numpy as jnp
from jax import lax
from jax.sharding import PartitionSpec as P

QH = 64
KVH = 8
HD = 128


def cut_along(array, dim, devices):
    lengths = array.shape
    tiles = array.reshape(*lengths[:dim], devices, lengths[dim] // devices, *lengths[dim + 1 :])
    return jnp.moveaxis(tiles, dim, 0)


def edges_of(length, count):
    step = length // count
    if step >= 8:
        step -= step % 8
    return [step * k for k in range(1, count)]


def joined_along(tiles, dim):
    lengths = list(tiles.shape[1:])
    lengths[dim] *= tiles.shape[0]
    return jnp.moveaxis(tiles, 0, dim).reshape(lengths)


def several_exchanges(array, axis, pieces, split_dim, concat_dim):
    tiles = cut_along(array, split_dim, lax.axis_size(axis))
    split_at = max(range(1, max(2, tiles.ndim - 1)), key=lambda d: tiles.shape[d])
    done = []
    for piece in jnp.split(tiles, edges_of(tiles.shape[split_at], pieces), axis=split_at):
        if piece.size:
            done.append(lax.all_to_all(piece, axis, split_axis=0, concat_axis=0, tiled=True))
    return joined_along(jnp.concatenate(done, axis=split_at), concat_dim)


def sent_and_summed(array, axis, dim):
    devices = lax.axis_size(axis)
    tiles = lax.all_to_all(cut_along(array, dim, devices), axis, 0, 0, tiled=True)
    return jnp.sum(tiles, axis=0)


def in_one_piece(arrays, axis, dim, along):
    ends, at = ([], 0)
    for a in arrays[:-1]:
        at += a.shape[along]
        ends.append(at)
    both = jnp.concatenate(arrays, axis=along)
    return tuple(jnp.split(sent_and_summed(both, axis, dim), ends, axis=along))


def attend_slots(queries, prompt_kv, suffix_kv, fresh, lengths, prompt_ids):
    samples = queries.shape[0]
    kv_heads = suffix_kv.shape[3] // HD
    share = QH // KVH
    prompt_len = prompt_kv.shape[1]
    suffix_cap = suffix_kv.shape[1]
    chooser = (prompt_ids[:, None] == jnp.arange(prompt_kv.shape[0])[None, :]).astype(jnp.bfloat16)
    chosen = jnp.einsum(
        "sp,pltw->sltw", chooser, prompt_kv, preferred_element_type=jnp.float32
    ).astype(jnp.bfloat16)
    key_rows = jnp.concatenate([chosen[:, :, 0], suffix_kv[:, :, 0]], 1).reshape(
        samples, -1, kv_heads, HD
    )
    value_rows = jnp.concatenate([chosen[:, :, 1], suffix_kv[:, :, 1]], 1).reshape(
        samples, -1, kv_heads, HD
    )
    heads = queries.reshape(samples, kv_heads, share, HD)
    scale = HD ** (-0.5)
    scores = (
        jnp.einsum("skgd,slkd->skgl", heads, key_rows, preferred_element_type=jnp.float32) * scale
    )
    fresh_keys = fresh[:, 0].reshape(samples, kv_heads, HD)
    own_score = (
        jnp.einsum("skgd,skd->skg", heads, fresh_keys, preferred_element_type=jnp.float32) * scale
    )
    valid = jnp.concatenate(
        [jnp.ones((samples, prompt_len), bool), jnp.arange(suffix_cap)[None, :] < lengths[:, None]],
        1,
    )
    scores = jnp.where(valid[:, None, None, :], scores, -1e30)
    highest = jnp.maximum(jnp.max(scores, -1), own_score)
    spread = jnp.exp(scores - highest[..., None])
    own_spread = jnp.exp(own_score - highest)
    total = jnp.sum(spread, -1) + own_spread
    weights = (spread / total[..., None]).astype(jnp.bfloat16)
    own_weight = (own_spread / total).astype(jnp.bfloat16)
    mixed = jnp.einsum("skgl,slkd->skgd", weights, value_rows, preferred_element_type=jnp.float32)
    fresh_values = fresh[:, 1].reshape(samples, kv_heads, 1, HD).astype(jnp.float32)
    mixed = mixed + own_weight.astype(jnp.float32)[..., None] * fresh_values
    live = prompt_ids >= 0
    return jnp.where(live[:, None], mixed.reshape(samples, -1), 0.0).astype(jnp.bfloat16)


def pick_field(hit, move_rows, column):
    return jnp.sum(jnp.where(hit, move_rows[:, column], 0))


def per_device(
    suffix_cache,
    prompt_cache,
    query_first,
    fresh_first,
    query_second,
    fresh_second,
    out_weight,
    suffix_len,
    prompt_slot,
    moves,
):
    slot_count = suffix_cache.shape[0]
    suffix_cap = suffix_cache.shape[1]
    own_group = lax.axis_index("grp")
    row_base = own_group * slot_count
    lengths = lax.dynamic_slice_in_dim(suffix_len, row_base, slot_count)
    attn_first = attend_slots(
        query_first, prompt_cache, suffix_cache, fresh_first, lengths, prompt_slot
    )
    positions = jnp.arange(suffix_cap)
    write_mask = (positions[None, :] == lengths[:, None]) & (prompt_slot[:, None] >= 0)
    appended = jnp.where(write_mask[:, :, None, None], fresh_first[:, None], suffix_cache)
    source_hit = moves[:, 0] == own_group
    target_hit = moves[:, 2] == own_group
    is_source = jnp.any(source_hit)
    is_target = jnp.any(target_hit)
    out_slot = pick_field(source_hit, moves, 1)
    destination = pick_field(source_hit, moves, 2)
    in_source = pick_field(target_hit, moves, 0)
    in_from_slot = pick_field(target_hit, moves, 1)
    in_slot = pick_field(target_hit, moves, 3)
    in_prompt = pick_field(target_hit, moves, 4)
    sample_rows = lax.dynamic_index_in_dim(appended, out_slot, 0, keepdims=False)
    prompt_index = jnp.maximum(
        lax.dynamic_index_in_dim(prompt_slot, out_slot, 0, keepdims=False), 0
    )
    prompt_rows = lax.dynamic_index_in_dim(prompt_cache, prompt_index, 0, keepdims=False)
    packed = jnp.concatenate([sample_rows, prompt_rows], 0)
    peer_count = lax.axis_size("grp")
    lane_mask = (jnp.arange(peer_count) == destination) & is_source
    outgoing = jnp.where(lane_mask[:, None, None, None], packed[None], jnp.zeros((), jnp.bfloat16))
    received = several_exchanges(outgoing, "grp", 2, 0, 0)
    arrived = lax.dynamic_index_in_dim(received, in_source, 0, keepdims=False)
    suffix_in = arrived[:suffix_cap]
    prompt_in = arrived[suffix_cap:]
    slot_ids = jnp.arange(slot_count)
    into_slot = (slot_ids == in_slot) & is_target
    leaving = (slot_ids == out_slot) & is_source
    suffix_moved = jnp.where(into_slot[:, None, None, None], suffix_in[None], appended)
    into_prompt = (jnp.arange(prompt_cache.shape[0]) == in_prompt) & is_target
    prompt_moved = jnp.where(into_prompt[:, None, None, None], prompt_in[None], prompt_cache)
    in_length = (
        lax.dynamic_index_in_dim(
            suffix_len, in_source * slot_count + in_from_slot, 0, keepdims=False
        )
        + 1
    )
    grown = jnp.where(prompt_slot >= 0, lengths + 1, 0)
    length_moved = jnp.where(into_slot, in_length, jnp.where(leaving, 0, grown))
    slot_moved = jnp.where(into_slot, in_prompt, jnp.where(leaving, -1, prompt_slot))
    attn_second = attend_slots(
        query_second, prompt_moved, suffix_moved, fresh_second, length_moved, slot_moved
    )
    proj_first = jnp.dot(attn_first, out_weight, preferred_element_type=jnp.float32)
    proj_second = jnp.dot(attn_second, out_weight, preferred_element_type=jnp.float32)
    out_first, out_second = in_one_piece((proj_first, proj_second), "tp", 1, 0)
    return (out_first.astype(jnp.bfloat16), out_second.astype(jnp.bfloat16))


def solution(mesh):
    placed = (
        P("grp", None, None, "tp"),
        P("grp", None, None, "tp"),
        P("grp", "tp"),
        P("grp", None, "tp"),
        P("grp", "tp"),
        P("grp", None, "tp"),
        P("tp", None),
        P(),
        P("grp"),
        P(),
    )
    return jax.shard_map(
        per_device,
        mesh=mesh,
        in_specs=placed,
        out_specs=(P("grp", "tp"), P("grp", "tp")),
        check_vma=False,
    )
```

profile of v0, /device:TPU:1, one launch (start us, length us, event | category | flops | bytes accessed | tf_op | source)
XLA Modules:
  0.0 441.6 jit_solution(18149206590518729838)
XLA Ops:
  0.6 1.1 slice_reduce_fusion.2
  1.8 0.6 fusion.58
  2.4 0.8 select_reduce_fusion.1
  5.6 1.2 dynamic_slice.24
  7.4 0.6 reduce_or.18
  8.1 3.7 broadcast_compare_fusion.2
  11.8 2.0 select_select_fusion
  13.7 0.1 iota_compare_fusion.2
  13.8 0.2 copy.30
  14.0 0.7 copy.31
  15.3 1.2 dynamic_slice.26
  16.5 3.4 fusion.60
  19.9 0.5 constant_dynamic-slice_fusion.1
  21.1 1.1 constant_dynamic-slice_fusion
  22.2 1.3 compare_and_fusion
  23.6 1.9 broadcast_select_fusion
  25.5 4.3 fusion.59
  29.8 195.2 %all_to_all.15 = bf16[32,1,512,2,128]{4,2,3,1,0:T(8,128)(2,1)} all-to-all(bf16[32,1,512,2,128]{4,2,3,1,0:T(8,128)(2,1)S(1)} %get-tuple-element.20), channel_id=1, replica_groups=mesh['grp'=32,'tp'=8] {'grp'}, dimensions={0} | all-to-all | bytes 16777216 | tf_op jit(solution)/shard_map/all_to_all | solution.py:36
  225.0 0.0 copy-start
  225.0 0.0 copy-start.2
  225.0 6.8 %all-to-all-start.1 = ((bf16[32,1,512,2,128]{4,2,3,1,0:T(8,128)(2,1)}), bf16[32,1,512,2,128]{4,2,3,1,0:T(8,128)(2,1)}, u32[]{:S(2)}, u32[]{:S(2)}) async-start(bf16[32,1,512,2,128]{4,2,3,1,0:T(8,128)(2,1)} %get-tuple-element.19), calls=%async_computation.1 | async-start | bytes 16777216 | tf_op jit(solution)/shard_map/all_to_all | solution.py:36
  231.9 0.0 copy-start.1
  231.9 0.0 copy-start.4
  231.9 0.0 copy-start.3
  231.9 0.0 copy-start.5
  233.9 1.2 compare_and_fusion.1
  235.1 0.4 slice_bitcast_fusion.6
  235.4 0.0 copy-done
  235.5 0.0 copy-done.2
  235.5 1.6 convolution_convert_fusion.1
  237.1 0.4 slice_bitcast_fusion.7
  237.4 0.7 pad_maximum_fusion
  238.1 0.0 copy-done.1
  238.1 0.0 copy-done.4
  238.1 0.1 fusion.28
  238.3 0.5 fusion.63
  238.7 0.2 fusion.13
  238.9 0.7 pad_maximum_fusion.1
  239.6 0.3 fusion.5
  240.0 0.0 copy-done.3
  240.0 0.0 copy-done.5
  240.0 0.1 fusion.25
  240.1 4.6 %fusion.21 = f32[4,4096]{1,0:T(4,128)S(1)} fusion(bf16[1024,4096]{1,0:T(8,128)(2,1)} %param.16, bf16[1,4,8,128]{3,2,1,0:T(8,128)(2,1)S(1)} %fusion.5, pred[4]{0:T(512)(128)(4,1)S(1)} %get-tuple-element.41), kind=kOutput, calls=%fused_computation.57 | convolution fusion | flops 33558528 | bytes 8462340 | tf_op jit(solution)/shard_map/dot_general | solution.py:166
  244.7 176.6 %all-to-all-done.1 = bf16[32,1,512,2,128]{4,2,3,1,0:T(8,128)(2,1)} async-done(((bf16[32,1,512,2,128]{4,2,3,1,0:T(8,128)(2,1)}), bf16[32,1,512,2,128]{4,2,3,1,0:T(8,128)(2,1)}, u32[]{:S(2)}, u32[]{:S(2)}) %all-to-all-start.1) | async-done | bytes 8388640 | tf_op jit(solution)/shard_map/all_to_all | solution.py:36
  421.4 1.1 fusion.10
  422.5 0.3 copy.34
  422.7 0.6 broadcast_select_fusion.2
  423.4 0.0 slice-start
  423.4 1.6 convolution_convert_fusion
  425.0 0.4 slice_bitcast_fusion.3
  425.3 0.6 broadcast_select_fusion.1
  426.0 0.0 slice-start.1
  426.0 0.4 slice_bitcast_fusion.2
  426.4 0.7 pad_maximum_fusion.2
  427.1 0.5 fusion.62
  427.5 0.2 fusion.14
  427.7 0.7 pad_maximum_fusion.3
  428.4 0.3 fusion.4
  428.8 0.0 slice-done
  428.8 0.0 slice-done.1
  428.8 1.2 fusion.23
  430.1 10.9 %all_to_all.16 = f32[8,8,512]{2,1,0:T(8,128)S(1)} all-to-all(f32[8,8,512]{2,1,0:T(8,128)S(1)} %bitcast.95), channel_id=1, replica_groups=mesh['grp'=32,'tp'=8] {'tp'}, dimensions={0} | all-to-all | bytes 262144 | tf_op jit(solution)/shard_map/all_to_all | solution.py:42
  441.0 0.6 fusion.61
  (15 shorter events, 0.3 us)
Async XLA Ops:
  225.0 10.4 %copy-start = (bf16[2,512,2,128]{3,2,1,0:T(2,128)(2,1)S(1)}, bf16[2,512,2,128]{3,2,1,0:T(2,128)(2,1)}, u32[]{:S(2)}) copy-start(bf16[2,512,2,128]{3,2,1,0:T(2,128)(2,1)} %param.11) | copy-start | bytes 1572868
  225.0 10.4 %copy-start.2 = (s32[4]{0:T(128)S(1)}, s32[4]{0:T(128)}, u32[]{:S(2)}) copy-start(s32[4]{0:T(128)} %param.18) | copy-start | bytes 52
  225.0 196.3 %all-to-all-start.1 = ((bf16[32,1,512,2,128]{4,2,3,1,0:T(8,128)(2,1)}), bf16[32,1,512,2,128]{4,2,3,1,0:T(8,128)(2,1)}, u32[]{:S(2)}, u32[]{:S(2)}) async-start(bf16[32,1,512,2,128]{4,2,3,1,0:T(8,128)(2,1)} %get-tuple-element.19), calls=%async_computation.1 | async-start | bytes 16777216 | tf_op jit(solution)/shard_map/all_to_all | solution.py:36
  231.9 6.2 %copy-start.1 = (bf16[4,2,128]{2,1,0:T(2,128)(2,1)S(1)}, bf16[4,2,128]{2,1,0:T(2,128)(2,1)}, u32[]{:S(2)}) copy-start(bf16[4,2,128]{2,1,0:T(2,128)(2,1)} %param.13) | copy-start | bytes 6148
  231.9 6.2 %copy-start.4 = (bf16[4,1024]{1,0:T(4,128)(2,1)S(1)}, bf16[4,1024]{1,0:T(4,128)(2,1)}, u32[]{:S(2)}) copy-start(bf16[4,1024]{1,0:T(4,128)(2,1)} %param.12) | copy-start | bytes 24580
  231.9 8.1 %copy-start.3 = (bf16[4,2,128]{2,1,0:T(2,128)(2,1)S(1)}, bf16[4,2,128]{2,1,0:T(2,128)(2,1)}, u32[]{:S(2)}) copy-start(bf16[4,2,128]{2,1,0:T(2,128)(2,1)} %param.15) | copy-start | bytes 6148
  231.9 8.1 %copy-start.5 = (bf16[4,1024]{1,0:T(4,128)(2,1)S(1)}, bf16[4,1024]{1,0:T(4,128)(2,1)}, u32[]{:S(2)}) copy-start(bf16[4,1024]{1,0:T(4,128)(2,1)} %param.14) | copy-start | bytes 24580
  423.4 5.4 %slice-start = ((s8[8388608]{0:T(1024)(128)(4,1)}), s8[4194304]{0:T(1024)(128)(4,1)S(1)}, s32[]{:S(2)}) async-start(s8[8388608]{0:T(1024)(128)(4,1)} %bitcast.91), calls=%async_computation.3 | async-start | bytes 8388608
  426.0 2.8 slice-start.1
where the time goes:
time: 442 us
  blocking collectives  206 us (47%)
  waiting for transfers between devices  177 us (40%)
  other arithmetic  21.1 us (5%)
  local copies, waits for them, and re-layouts  13 us (3%)
  matrix products  10.8 us (2%)
  between operations  7.05 us (2%)
  starting transfers between devices  6.83 us (2%)
    all_to_all x1, blocking collectives, several_exchanges(): lax.all_to_all(piece, axis, split_axis=0, concat_axis=0, tiled=True)  195 us
    all_to_all x1, waiting for transfers between devices, several_exchanges(): lax.all_to_all(piece, axis, split_axis=0, concat_axis=0, tiled=True)  177 us
    all_to_all x1, blocking collectives, sent_and_summed(): lax.all_to_all(cut_along(array, dim, devices), axis, 0, 0, tiled=True)  10.9 us
  transfers between devices with their start and end apart: 1, of which 1 were waited for; matrix products, arithmetic and copies ran while one was open for 2% of the time, Pallas kernels for 0%

commit v1 on v0

v1 whole, which is shorter than its diff:
```python
import jax
import jax.numpy as jnp
from jax import lax
from jax.experimental import pallas as pl
from jax.experimental.pallas import tpu as pltpu
from jax.sharding import PartitionSpec as P

QH = 64
KVH = 8
HD = 128
HEADS = QH // KVH

BF = jnp.bfloat16
F32 = jnp.float32
SMEM = pl.BlockSpec(memory_space=pltpu.SMEM)
VMEM = pl.BlockSpec(memory_space=pltpu.VMEM)


def empty_slot_of(slot_ref):
    found = jnp.int32(0)
    for s in range(slot_ref.shape[0]):
        found = jnp.where(slot_ref[s] < 0, jnp.int32(s), found)
    return found


def look_up(moves_ref, own, key, fields):
    hit_any = jnp.int32(0)
    values = [jnp.int32(0) for _ in fields]
    for i in range(moves_ref.shape[0]):
        hit = moves_ref[i, key] == own
        hit_any = jnp.where(hit, jnp.int32(1), hit_any)
        values = [jnp.where(hit, moves_ref[i, f], v) for f, v in zip(fields, values)]
    return hit_any, values


def offer_kernel(slot_ref, query_ref, fresh_ref, out_ref):
    empty = empty_slot_of(slot_ref)
    slots = query_ref.shape[0]
    mine = lax.broadcasted_iota(jnp.int32, (slots, HD), 0) == empty
    rows = []
    for h in range(HEADS):
        part = query_ref[:, h * HD : (h + 1) * HD].astype(F32)
        rows.append(jnp.sum(jnp.where(mine, part, 0.0), axis=0, keepdims=True))
    pair = jnp.zeros((2, HD), F32)
    for s in range(slots):
        pair = jnp.where(empty == s, fresh_ref[s].astype(F32), pair)
    rows += [pair, jnp.zeros((6, HD), F32)]
    block = jnp.concatenate(rows, axis=0).astype(BF)
    out_ref[...] = jnp.broadcast_to(block[None], out_ref.shape)


def attend_kernel(
    own_ref,
    len_ref,
    slot_ref,
    moves_ref,
    query_first_ref,
    query_second_ref,
    fresh_first_ref,
    fresh_second_ref,
    offers_ref,
    prompt_ref,
    suffix_ref,
    rows_ref,
    moved_ref,
    queries_ref,
):
    own = own_ref[0]
    slots = query_first_ref.shape[0]
    prompt_width = prompt_ref.shape[1]
    suffix_width = suffix_ref.shape[1]
    is_source, (out_slot, destination) = look_up(moves_ref, own, 0, (1, 2))
    for h in range(HEADS):
        queries_ref[:, h, :] = query_first_ref[:, h * HD : (h + 1) * HD].astype(F32)
        queries_ref[:, HEADS + h, :] = query_second_ref[:, h * HD : (h + 1) * HD].astype(F32)
    offer = offers_ref[destination].astype(F32)
    scale = HD ** (-0.5)
    second_row = lax.broadcasted_iota(jnp.int32, (2 * HEADS, 1), 0) >= HEADS
    prompt_keys = lax.broadcasted_iota(jnp.int32, (2 * HEADS, prompt_width), 1) % 2 == 0
    column = lax.broadcasted_iota(jnp.int32, (2 * HEADS, suffix_width), 1)
    suffix_keys = column % 2 == 0
    moved = jnp.zeros((HEADS, HD), F32)
    contract_last = (((1,), (1,)), ((), ()))
    for s in range(slots):
        leaving = (is_source == 1) & (out_slot == s)
        length = len_ref[own * slots + s]
        prompt_id = slot_ref[s]
        live = prompt_id >= 0
        first = queries_ref[s, :HEADS, :]
        second = jnp.where(leaving, offer[:HEADS], queries_ref[s, HEADS:, :])
        both = jnp.concatenate([first, second], axis=0)
        pair_first = fresh_first_ref[s].astype(F32)
        pair_second = jnp.where(leaving, offer[HEADS : HEADS + 2], fresh_second_ref[s].astype(F32))
        queries = both.astype(BF)
        prompt = prompt_ref[jnp.maximum(prompt_id, 0)]
        suffix = suffix_ref[s]
        on_prompt = (
            lax.dot_general(queries, prompt, contract_last, preferred_element_type=F32) * scale
        )
        on_suffix = (
            lax.dot_general(queries, suffix, contract_last, preferred_element_type=F32) * scale
        )
        on_prompt = jnp.where(prompt_keys, on_prompt, -1e30)
        on_suffix = jnp.where(suffix_keys & (column < 2 * length), on_suffix, -1e30)
        on_first = jnp.sum(both * pair_first[0:1], axis=1, keepdims=True) * scale
        on_second = jnp.sum(both * pair_second[0:1], axis=1, keepdims=True) * scale
        on_second = jnp.where(second_row, on_second, -1e30)
        highest = jnp.maximum(
            jnp.max(on_prompt, axis=1, keepdims=True), jnp.max(on_suffix, axis=1, keepdims=True)
        )
        highest = jnp.maximum(highest, jnp.maximum(on_first, on_second))
        prompt_spread = jnp.exp(on_prompt - highest)
        suffix_spread = jnp.exp(on_suffix - highest)
        first_spread = jnp.exp(on_first - highest)
        second_spread = jnp.exp(on_second - highest)
        total = (
            jnp.sum(prompt_spread, axis=1, keepdims=True)
            + jnp.sum(suffix_spread, axis=1, keepdims=True)
            + first_spread
            + second_spread
        )
        share = 1.0 / total
        prompt_weights = pltpu.roll(prompt_spread * share, 1, 1).astype(BF)
        suffix_weights = pltpu.roll(suffix_spread * share, 1, 1).astype(BF)
        mixed = lax.dot(prompt_weights, prompt, preferred_element_type=F32)
        mixed += lax.dot(suffix_weights, suffix, preferred_element_type=F32)
        mixed += (first_spread * share).astype(BF).astype(F32) * pair_first[1:2]
        mixed += (second_spread * share).astype(BF).astype(F32) * pair_second[1:2]
        mixed = mixed.astype(BF).astype(F32)
        stays = live & jnp.logical_not(leaving)
        rows_ref[:, s, :] = jnp.where(live, mixed[:HEADS], 0.0)
        rows_ref[:, slots + s, :] = jnp.where(stays, mixed[HEADS:], 0.0)
        moved = jnp.where(leaving, mixed[HEADS:], moved)
    moved_ref[...] = jnp.broadcast_to(moved.astype(BF)[None], moved_ref.shape)


def project_kernel(own_ref, slot_ref, moves_ref, rows_ref, arrived_ref, weight_ref, out_ref):
    own = own_ref[0]
    slots = slot_ref.shape[0]
    is_target, (in_source,) = look_up(moves_ref, own, 2, (0,))
    row = jnp.where(is_target == 1, slots + empty_slot_of(slot_ref), -1)
    arrived = arrived_ref[in_source].astype(F32)
    into = lax.broadcasted_iota(jnp.int32, (2 * slots, HD), 0) == row
    parts = [jnp.where(into, arrived[h : h + 1], rows_ref[h]) for h in range(HEADS)]
    rows = jnp.concatenate(parts, axis=1).astype(BF)
    width = out_ref.shape[2]
    for t in range(out_ref.shape[0]):
        out_ref[t] = lax.dot(
            rows, weight_ref[:, t * width : (t + 1) * width], preferred_element_type=F32
        )


def sum_kernel(parts_ref, first_ref, second_ref):
    total = jnp.sum(parts_ref[...], axis=0)
    slots = first_ref.shape[0]
    first_ref[...] = total[:slots].astype(BF)
    second_ref[...] = total[slots:].astype(BF)


def per_device(
    suffix_cache,
    prompt_cache,
    query_first,
    fresh_first,
    query_second,
    fresh_second,
    out_weight,
    suffix_len,
    prompt_slot,
    moves,
):
    slots, cap = suffix_cache.shape[:2]
    prompts, prompt_len = prompt_cache.shape[:2]
    groups = lax.axis_size("grp")
    shares = lax.axis_size("tp")
    features = out_weight.shape[1]
    own = lax.axis_index("grp").astype(jnp.int32).reshape(1)
    suffix_rows = suffix_cache.reshape(slots, 2 * cap, HD)
    prompt_rows = prompt_cache.reshape(prompts, 2 * prompt_len, HD)
    offer = pl.pallas_call(
        offer_kernel,
        out_shape=jax.ShapeDtypeStruct((groups, 2 * HEADS, HD), BF),
        in_specs=[SMEM, VMEM, VMEM],
        out_specs=VMEM,
        name="offer",
    )(prompt_slot, query_second, fresh_second)
    offers = lax.all_to_all(offer, "grp", 0, 0, tiled=True)
    rows, moved = pl.pallas_call(
        attend_kernel,
        out_shape=(
            jax.ShapeDtypeStruct((HEADS, 2 * slots, HD), F32),
            jax.ShapeDtypeStruct((groups, HEADS, HD), BF),
        ),
        in_specs=[SMEM, SMEM, SMEM, SMEM] + [VMEM] * 7,
        out_specs=(VMEM, VMEM),
        scratch_shapes=[pltpu.VMEM((slots, 2 * HEADS, HD), F32)],
        name="attend",
    )(
        own,
        suffix_len,
        prompt_slot,
        moves,
        query_first,
        query_second,
        fresh_first,
        fresh_second,
        offers,
        prompt_rows,
        suffix_rows,
    )
    arrived = lax.all_to_all(moved, "grp", 0, 0, tiled=True)
    parts = pl.pallas_call(
        project_kernel,
        out_shape=jax.ShapeDtypeStruct((shares, 2 * slots, features // shares), F32),
        in_specs=[SMEM, SMEM, SMEM, VMEM, VMEM, VMEM],
        out_specs=VMEM,
        name="project",
    )(own, prompt_slot, moves, rows, arrived, out_weight)
    parts = lax.all_to_all(parts, "tp", 0, 0, tiled=True)
    out = jax.ShapeDtypeStruct((slots, features // shares), BF)
    return pl.pallas_call(
        sum_kernel,
        out_shape=(out, out),
        in_specs=[VMEM],
        out_specs=(VMEM, VMEM),
        name="sum",
    )(parts)


def solution(mesh):
    placed = (
        P("grp", None, None, "tp"),
        P("grp", None, None, "tp"),
        P("grp", "tp"),
        P("grp", None, "tp"),
        P("grp", "tp"),
        P("grp", None, "tp"),
        P("tp", None),
        P(),
        P("grp"),
        P(),
    )
    return jax.shard_map(
        per_device,
        mesh=mesh,
        in_specs=placed,
        out_specs=(P("grp", "tp"), P("grp", "tp")),
        check_vma=False,
    )
```

time: 442 us -> 62 us (0.14)
  blocking collectives: 206 us -> 26.4 us
  waiting for transfers between devices: 177 us -> 9.34 us
  other arithmetic: 21.1 us -> 0 us
  Pallas kernels: 0 us -> 12.8 us
  local copies, waits for them, and re-layouts: 13 us -> 0.64 us
  matrix products: 10.8 us -> 0 us
  between operations: 7.05 us -> 0.65 us
  starting transfers between devices: 6.83 us -> 11.9 us
    all_to_all x2, blocking collectives: 206 us -> 26.4 us  [the longest x1 13.4 us: per_device(): arrived = lax.all_to_all(moved, 'grp', 0, 0, tiled=True)]
    all_to_all x1, waiting for transfers between devices: 177 us -> 9.34 us  [per_device(): offers = lax.all_to_all(offer, 'grp', 0, 0, tiled=True)]
    pallas_call x0 -> x4, Pallas kernels: none -> 12.8 us  [the longest x1 5.3 us: per_device(): pl.pallas_call(project_kernel, out_shape=jax.ShapeDtypeStruct((shares, 2...]
    dot_general x10 -> x0, matrix products: 10.8 us -> none  [the longest x1 4.61 us: per_device(): jnp.dot(attn_first, out_weight, preferred_element_type=jnp.float32)]
    select_n x4 -> x0, other arithmetic: 5.07 us -> none  [the longest x1 1.95 us: per_device(): length_moved = jnp.where(into_slot, in_length, jnp.where(leaving, 0, grown))]
    all_to_all x1, starting transfers between devices: 6.83 us -> 11.9 us  [per_device(): offers = lax.all_to_all(offer, 'grp', 0, 0, tiled=True)]
    split x2 -> x0, local copies, waits for them, and re-layouts: 4.9 us -> none  [the longest x1 4.3 us: several_exchanges(): jnp.split(tiles, edges_of(tiles.shape[split_at], pieces), axis=split_at)]
  transfers between devices with their start and end apart: 1 -> 1, of which waited for: 1 -> 1; matrix products, arithmetic and copies ran while one was open for 2% -> 0% of each run, Pallas kernels for 0% -> 0%
where the time goes in v1:
time: 62 us; the launch traced here: 61.6 us
  blocking collectives  26.4 us (43%)
  Pallas kernels  12.8 us (21%)
  starting transfers between devices  11.9 us (19%)
  waiting for transfers between devices  9.34 us (15%)
  between operations  0.65 us (1%)
  local copies, waits for them, and re-layouts  0.64 us (1%)
    all_to_all x1, blocking collectives, per_device(): arrived = lax.all_to_all(moved, 'grp', 0, 0, tiled=True)  13.4 us
    all_to_all x1, blocking collectives, per_device(): parts = lax.all_to_all(parts, 'tp', 0, 0, tiled=True)  13 us
    all_to_all x1, starting transfers between devices, per_device(): offers = lax.all_to_all(offer, 'grp', 0, 0, tiled=True)  11.9 us
    all_to_all x1, waiting for transfers between devices, per_device(): offers = lax.all_to_all(offer, 'grp', 0, 0, tiled=True)  9.34 us
    pallas_call x1, Pallas kernels, per_device(): pl.pallas_call(project_kernel, out_shape=jax.ShapeDtypeStruct((shares, 2...  5.3 us
    pallas_call x1, Pallas kernels, per_device(): pl.pallas_call(attend_kernel, out_shape=(jax.ShapeDtypeStruct((HEADS, 2 *...  4.57 us
    pallas_call x1, Pallas kernels, per_device(): pl.pallas_call(sum_kernel, out_shape=(out, out), in_specs=[VMEM], out_spe...  1.51 us
    pallas_call x1, Pallas kernels, per_device(): pl.pallas_call(offer_kernel, out_shape=jax.ShapeDtypeStruct((groups, 2 *...  1.38 us
  transfers between devices with their start and end apart: 1, of which 1 were waited for; matrix products, arithmetic and copies ran while one was open for 0% of the time, Pallas kernels for 0%

profile of v1, /device:TPU:1, one launch (start us, length us, event | category | flops | bytes accessed | tf_op | source)
XLA Modules:
  0.0 61.6 jit_solution(18113121449941236863)
XLA Ops:
  0.6 1.4 %offer.1 = bf16[32,16,128]{2,1,0:T(8,128)(2,1)} custom-call(s32[4]{0:T(128)} %slot_ref.5, bf16[4,1024]{1,0:T(4,128)(2,1)} %query_second_ref.1, bf16[4,2,128]{2,1,0:T(2,128)(2,1)} %fresh_second_ref.1), custom_call_target="tpu_custom_call" | custom-call | tf_op jit(solution)/shard_map/offer/pallas_call | solution.py:180
  2.0 11.9 %all-to-all-start = ((bf16[32,16,128]{2,1,0:T(8,128)(2,1)}), bf16[32,16,128]{2,1,0:T(8,128)(2,1)S(1)}, u32[]{:S(2)}, u32[]{:S(2)}) async-start(bf16[32,16,128]{2,1,0:T(8,128)(2,1)} %offer.1), calls=%async_computation | async-start | bytes 262144 | tf_op jit(solution)/shard_map/all_to_all | solution.py:187
  13.9 9.3 %all-to-all-done.offers_ref = bf16[32,16,128]{2,1,0:T(8,128)(2,1)S(1)} async-done(((bf16[32,16,128]{2,1,0:T(8,128)(2,1)}), bf16[32,16,128]{2,1,0:T(8,128)(2,1)S(1)}, u32[]{:S(2)}, u32[]{:S(2)}) %all-to-all-start) | async-done | bytes 131104 | tf_op jit(solution)/shard_map/all_to_all | solution.py:187
  23.2 0.0 copy-start
  23.2 0.6 %copy-done = bf16[32,16,128]{2,1,0:T(8,128)(2,1)} copy-done((bf16[32,16,128]{2,1,0:T(8,128)(2,1)}, bf16[32,16,128]{2,1,0:T(8,128)(2,1)S(1)}, u32[]{:S(2)}) %copy-start) | copy-done | bytes 131096
  23.9 4.6 %attend.1 = (f32[8,8,128]{2,1,0:T(8,128)}, bf16[32,8,128]{2,1,0:T(8,128)(2,1)}) custom-call(s32[1]{0:T(128)} %bitcast.own_ref, s32[128]{0:T(128)} %len_ref.1, s32[4]{0:T(128)} %slot_ref.5, s32[8,5]{1,0:T(8,128)} %moves_ref.3, bf16[4,1024]{1,0:T(4,128)(2,1)} %query_first_ref.1, bf16[4,1024]{1,0:T(4,128)(2,1)} %query_second_ref.1, ...), custom_call_target="tpu_custom_call" | custom-call | tf_op jit(solution)/shard_map/attend/pallas_call | solution.py:188
  28.4 13.4 %all_to_all.15.arrived_ref = bf16[32,8,128]{2,1,0:T(8,128)(2,1)} all-to-all(bf16[32,8,128]{2,1,0:T(8,128)(2,1)} %get-tuple-element.5), channel_id=1, replica_groups=mesh['grp'=32,'tp'=8] {'grp'}, dimensions={0} | all-to-all | bytes 131072 | tf_op jit(solution)/shard_map/all_to_all | solution.py:211
  41.8 5.3 %project.1 = f32[8,8,512]{2,1,0:T(8,128)} custom-call(s32[1]{0:T(128)} %bitcast.own_ref, s32[4]{0:T(128)} %slot_ref.5, s32[8,5]{1,0:T(8,128)} %moves_ref.3, f32[8,8,128]{2,1,0:T(8,128)} %get-tuple-element.4.rows_ref, bf16[32,8,128]{2,1,0:T(8,128)(2,1)} %all_to_all.15.arrived_ref, bf16[1024,4096]{1,0:T(8,128)(2,1)} %weight_ref.1), custom_call_target="tpu_custom_call" | custom-call | tf_op jit(solution)/shard_map/project/pallas_call | solution.py:212
  47.1 13.0 %all_to_all.16.parts_ref = f32[8,8,512]{2,1,0:T(8,128)} all-to-all(f32[8,8,512]{2,1,0:T(8,128)} %project.1), channel_id=1, replica_groups=mesh['grp'=32,'tp'=8] {'tp'}, dimensions={0} | all-to-all | bytes 262144 | tf_op jit(solution)/shard_map/all_to_all | solution.py:219
  60.1 1.5 %sum.1 = (bf16[4,512]{1,0:T(4,128)(2,1)}, bf16[4,512]{1,0:T(4,128)(2,1)}) custom-call(f32[8,8,512]{2,1,0:T(8,128)} %all_to_all.16.parts_ref), custom_call_target="tpu_custom_call" | custom-call | tf_op jit(solution)/shard_map/sum/pallas_call | solution.py:221
Async XLA Ops:
  2.0 21.2 %all-to-all-start = ((bf16[32,16,128]{2,1,0:T(8,128)(2,1)}), bf16[32,16,128]{2,1,0:T(8,128)(2,1)S(1)}, u32[]{:S(2)}, u32[]{:S(2)}) async-start(bf16[32,16,128]{2,1,0:T(8,128)(2,1)} %offer.1), calls=%async_computation | async-start | bytes 262144 | tf_op jit(solution)/shard_map/all_to_all | solution.py:187
  23.2 0.6 %copy-start = (bf16[32,16,128]{2,1,0:T(8,128)(2,1)}, bf16[32,16,128]{2,1,0:T(8,128)(2,1)S(1)}, u32[]{:S(2)}) copy-start(bf16[32,16,128]{2,1,0:T(8,128)(2,1)S(1)} %all-to-all-done.offers_ref) | copy-start | bytes 393220

commit v2 on v1

v2 whole, which is shorter than its diff:
```python
import jax
import jax.numpy as jnp
from jax import lax
from jax.experimental import pallas as pl
from jax.experimental.pallas import tpu as pltpu
from jax.sharding import PartitionSpec as P

QH = 64
KVH = 8
HD = 128
HEADS = QH // KVH

BF = jnp.bfloat16
F32 = jnp.float32
SMEM = pl.BlockSpec(memory_space=pltpu.SMEM)
VMEM = pl.BlockSpec(memory_space=pltpu.VMEM)


SMALL = pltpu.CompilerParams(vmem_limit_bytes=8 << 20)


def near(array):
    return pltpu.with_memory_space_constraint(array, pltpu.VMEM)


def empty_slot_of(slot_ref):
    found = jnp.int32(0)
    for s in range(slot_ref.shape[0]):
        found = jnp.where(slot_ref[s] < 0, jnp.int32(s), found)
    return found


def look_up(moves_ref, own, key, fields):
    hit_any = jnp.int32(0)
    values = [jnp.int32(0) for _ in fields]
    for i in range(moves_ref.shape[0]):
        hit = moves_ref[i, key] == own
        hit_any = jnp.where(hit, jnp.int32(1), hit_any)
        values = [jnp.where(hit, moves_ref[i, f], v) for f, v in zip(fields, values)]
    return hit_any, values


def offer_kernel(slot_ref, query_ref, fresh_ref, out_ref):
    empty = empty_slot_of(slot_ref)
    slots = query_ref.shape[0]
    mine = lax.broadcasted_iota(jnp.int32, (slots, HD), 0) == empty
    rows = []
    for h in range(HEADS):
        part = query_ref[:, h * HD : (h + 1) * HD].astype(F32)
        rows.append(jnp.sum(jnp.where(mine, part, 0.0), axis=0, keepdims=True))
    pair = jnp.zeros((2, HD), F32)
    for s in range(slots):
        pair = jnp.where(empty == s, fresh_ref[s].astype(F32), pair)
    rows += [pair, jnp.zeros((6, HD), F32)]
    block = jnp.concatenate(rows, axis=0).astype(BF)
    out_ref[...] = jnp.broadcast_to(block[None], out_ref.shape)


def attend(queries, cached, pairs):
    scale = HD ** (-0.5)
    narrow = queries.astype(BF)
    row = lax.broadcasted_iota(jnp.int32, (queries.shape[0], 1), 0)
    scores = []
    for rows, width in cached:
        score = (
            lax.dot_general(
                narrow, rows, (((1,), (1,)), ((), ())), preferred_element_type=F32
            )
            * scale
        )
        column = lax.broadcasted_iota(jnp.int32, score.shape, 1)
        counts = column % 2 == 0
        if width is not None:
            counts = counts & (column < width)
        scores.append(jnp.where(counts, score, -1e30))
    singles = []
    for pair, since in pairs:
        score = jnp.sum(queries * pair[0:1], axis=1, keepdims=True) * scale
        singles.append(jnp.where(row >= since, score, -1e30) if since else score)
    highest = singles[0]
    for score in singles[1:]:
        highest = jnp.maximum(highest, score)
    for score in scores:
        highest = jnp.maximum(highest, jnp.max(score, axis=1, keepdims=True))
    spreads = [jnp.exp(score - highest) for score in scores]
    single_spreads = [jnp.exp(score - highest) for score in singles]
    total = sum(single_spreads)
    for spread in spreads:
        total = total + jnp.sum(spread, axis=1, keepdims=True)
    share = 1.0 / total
    mixed = jnp.zeros(queries.shape, F32)
    for (rows, _), spread in zip(cached, spreads):
        weights = pltpu.roll(spread * share, 1, 1).astype(BF)
        mixed += lax.dot(weights, rows, preferred_element_type=F32)
    for (pair, _), spread in zip(pairs, single_spreads):
        mixed += (spread * share).astype(BF).astype(F32) * pair[1:2]
    return mixed.astype(BF)


def stay_kernel(
    own_ref,
    len_ref,
    slot_ref,
    moves_ref,
    query_first_ref,
    query_second_ref,
    fresh_first_ref,
    fresh_second_ref,
    prompt_ref,
    suffix_ref,
    rows_ref,
    kept_ref,
    pair_ref,
    facts_ref,
    queries_ref,
):
    own = own_ref[0]
    slots = query_first_ref.shape[0]
    is_source, (out_slot, destination) = look_up(moves_ref, own, 0, (1, 2))
    is_target, (in_source,) = look_up(moves_ref, own, 2, (0,))
    facts_ref[0] = destination
    facts_ref[1] = 2 * len_ref[own * slots + out_slot]
    facts_ref[2] = in_source
    facts_ref[3] = jnp.where(is_target == 1, slots + empty_slot_of(slot_ref), -1)
    for h in range(HEADS):
        queries_ref[:, h, :] = query_first_ref[:, h * HD : (h + 1) * HD].astype(F32)
        queries_ref[:, HEADS + h, :] = query_second_ref[:, h * HD : (h + 1) * HD].astype(F32)
    half = prompt_ref.shape[1]
    kept_ref[:half] = prompt_ref[jnp.maximum(slot_ref[out_slot], 0)]
    kept_ref[half:] = suffix_ref[out_slot]
    pair_ref[...] = fresh_first_ref[out_slot].astype(F32)
    for s in range(slots):
        prompt_id = slot_ref[s]
        live = prompt_id >= 0
        stays = live & jnp.logical_not((is_source == 1) & (out_slot == s))
        mixed = attend(
            queries_ref[s],
            (
                (prompt_ref[jnp.maximum(prompt_id, 0)], None),
                (suffix_ref[s], 2 * len_ref[own * slots + s]),
            ),
            ((fresh_first_ref[s].astype(F32), 0), (fresh_second_ref[s].astype(F32), HEADS)),
        ).astype(F32)
        rows_ref[:, s, :] = jnp.where(live, mixed[:HEADS], 0.0)
        rows_ref[:, slots + s, :] = jnp.where(stays, mixed[HEADS:], 0.0)


def leave_kernel(facts_ref, offers_ref, kept_ref, pair_ref, moved_ref):
    offer = offers_ref[facts_ref[0]].astype(F32)
    half = kept_ref.shape[0] // 2
    mixed = attend(
        offer[:HEADS],
        ((kept_ref[:half], None), (kept_ref[half:], facts_ref[1])),
        ((pair_ref[...], 0), (offer[HEADS : HEADS + 2], 0)),
    )
    moved_ref[...] = jnp.broadcast_to(mixed[None], moved_ref.shape)


def merge_kernel(facts_ref, rows_ref, arrived_ref, out_ref):
    arrived = arrived_ref[facts_ref[2]].astype(F32)
    into = lax.broadcasted_iota(jnp.int32, rows_ref.shape[1:], 0) == facts_ref[3]
    for h in range(HEADS):
        row = jnp.where(into, arrived[h : h + 1], rows_ref[h])
        out_ref[:, h * HD : (h + 1) * HD] = row.astype(BF)


def sum_kernel(parts_ref, first_ref, second_ref):
    total = jnp.sum(parts_ref[...], axis=0)
    slots = first_ref.shape[0]
    first_ref[...] = total[:slots].astype(BF)
    second_ref[...] = total[slots:].astype(BF)


def per_device(
    suffix_cache,
    prompt_cache,
    query_first,
    fresh_first,
    query_second,
    fresh_second,
    out_weight,
    suffix_len,
    prompt_slot,
    moves,
):
    slots, cap = suffix_cache.shape[:2]
    prompts, prompt_len = prompt_cache.shape[:2]
    groups = lax.axis_size("grp")
    shares = lax.axis_size("tp")
    features = out_weight.shape[1]
    own = lax.axis_index("grp").astype(jnp.int32).reshape(1)
    suffix_rows = suffix_cache.reshape(slots, 2 * cap, HD)
    prompt_rows = prompt_cache.reshape(prompts, 2 * prompt_len, HD)
    offer = pl.pallas_call(
        offer_kernel,
        out_shape=pltpu.VMEM((groups, 2 * HEADS, HD), BF),
        in_specs=[SMEM, VMEM, VMEM],
        out_specs=VMEM,
        name="offer",
    )(prompt_slot, query_second, fresh_second)
    offers = lax.all_to_all(offer, "grp", 0, 0, tiled=True)
    rows, kept, pair, facts = pl.pallas_call(
        stay_kernel,
        out_shape=(
            pltpu.VMEM((HEADS, 2 * slots, HD), F32),
            pltpu.VMEM((2 * cap + 2 * prompt_len, HD), BF),
            pltpu.VMEM((2, HD), F32),
            jax.ShapeDtypeStruct((4,), jnp.int32),
        ),
        in_specs=[SMEM] * 4 + [VMEM] * 6,
        out_specs=(VMEM, VMEM, VMEM, SMEM),
        scratch_shapes=[pltpu.VMEM((slots, 2 * HEADS, HD), F32)],
        name="stay",
    )(
        own,
        suffix_len,
        prompt_slot,
        moves,
        query_first,
        query_second,
        fresh_first,
        fresh_second,
        prompt_rows,
        suffix_rows,
    )
    moved = pl.pallas_call(
        leave_kernel,
        out_shape=pltpu.VMEM((groups, HEADS, HD), BF),
        in_specs=[SMEM, VMEM, VMEM, VMEM],
        out_specs=VMEM,
        compiler_params=SMALL,
        name="leave",
    )(facts, near(offers), near(kept), near(pair))
    arrived = lax.all_to_all(moved, "grp", 0, 0, tiled=True)
    merged = pl.pallas_call(
        merge_kernel,
        out_shape=pltpu.VMEM((2 * slots, HEADS * HD), BF),
        in_specs=[SMEM, VMEM, VMEM],
        out_specs=VMEM,
        compiler_params=SMALL,
        name="merge",
    )(facts, near(rows), near(arrived))
    parts = jnp.dot(merged, out_weight, preferred_element_type=F32)
    parts = parts.reshape(2 * slots, shares, features // shares).swapaxes(0, 1)
    parts = lax.all_to_all(parts, "tp", 0, 0, tiled=True)
    out = jax.ShapeDtypeStruct((slots, features // shares), BF)
    return pl.pallas_call(
        sum_kernel,
        out_shape=(out, out),
        in_specs=[VMEM],
        out_specs=(VMEM, VMEM),
        compiler_params=SMALL,
        name="sum",
    )(near(parts))


def solution(mesh):
    placed = (
        P("grp", None, None, "tp"),
        P("grp", None, None, "tp"),
        P("grp", "tp"),
        P("grp", None, "tp"),
        P("grp", "tp"),
        P("grp", None, "tp"),
        P("tp", None),
        P(),
        P("grp"),
        P(),
    )
    return jax.shard_map(
        per_device,
        mesh=mesh,
        in_specs=placed,
        out_specs=(P("grp", "tp"), P("grp", "tp")),
        check_vma=False,
    )
```

time: 62 us -> 56.2 us (0.906)
  Pallas kernels: 12.8 us -> 8.03 us
  matrix products: 0 us -> 4.58 us
  waiting for transfers between devices: 9.34 us -> 5.06 us
  blocking collectives: 26.4 us -> 25 us
    dot_general x0 -> x1, matrix products: none -> 4.58 us  [per_device(): parts = jnp.dot(merged, out_weight, preferred_element_type=F32)]
    all_to_all x1, waiting for transfers between devices: 9.34 us -> 5.06 us  [per_device(): offers = lax.all_to_all(offer, 'grp', 0, 0, tiled=True)]
    pallas_call x3 -> x4, Pallas kernels: 11.3 us -> 7.42 us  [the longest x1 4.27 us: per_device(): pl.pallas_call(stay_kernel, out_shape=(pltpu.VMEM((HEADS, 2 * slots, HD),...]
    pallas_call x1, Pallas kernels: 1.51 us -> 0.61 us  [per_device(): pl.pallas_call(sum_kernel, out_shape=(out, out), in_specs=[VMEM], out_spe...]
    all_to_all x1, blocking collectives: 13 us -> 12.2 us  [per_device(): parts = lax.all_to_all(parts, 'tp', 0, 0, tiled=True)]
  transfers between devices with their start and end apart: 1 -> 1, of which waited for: 1 -> 1; matrix products, arithmetic and copies ran while one was open for 0% -> 0% of each run, Pallas kernels for 0% -> 8%
where the time goes in v2:
time: 56.2 us; the launch traced here: 55.8 us
  blocking collectives  25 us (44%)
  starting transfers between devices  11.9 us (21%)
  Pallas kernels  8.03 us (14%)
  waiting for transfers between devices  5.06 us (9%)
  matrix products  4.58 us (8%)
  between operations  0.67 us (1%)
  local copies, waits for them, and re-layouts  0.66 us (1%)
    all_to_all x1, blocking collectives, per_device(): arrived = lax.all_to_all(moved, 'grp', 0, 0, tiled=True)  12.8 us
    all_to_all x1, blocking collectives, per_device(): parts = lax.all_to_all(parts, 'tp', 0, 0, tiled=True)  12.2 us
    all_to_all x1, starting transfers between devices, per_device(): offers = lax.all_to_all(offer, 'grp', 0, 0, tiled=True)  11.9 us
    all_to_all x1, waiting for transfers between devices, per_device(): offers = lax.all_to_all(offer, 'grp', 0, 0, tiled=True)  5.06 us
    dot_general x1, matrix products, per_device(): parts = jnp.dot(merged, out_weight, preferred_element_type=F32)  4.58 us
    pallas_call x1, Pallas kernels, per_device(): pl.pallas_call(stay_kernel, out_shape=(pltpu.VMEM((HEADS, 2 * slots, HD),...  4.27 us
    pallas_call x1, Pallas kernels, per_device(): pl.pallas_call(offer_kernel, out_shape=pltpu.VMEM((groups, 2 * HEADS, HD)...  1.38 us
    pallas_call x1, Pallas kernels, per_device(): pl.pallas_call(leave_kernel, out_shape=pltpu.VMEM((groups, HEADS, HD), BF...  1.21 us
  transfers between devices with their start and end apart: 1, of which 1 were waited for; matrix products, arithmetic and copies ran while one was open for 0% of the time, Pallas kernels for 8%

profile of v2, /device:TPU:1, one launch (start us, length us, event | category | flops | bytes accessed | tf_op | source)
XLA Modules:
  0.0 55.8 jit_solution(12708012906356570051)
XLA Ops:
  0.6 1.4 %offer.1 = bf16[32,16,128]{2,1,0:T(8,128)(2,1)} custom-call(s32[4]{0:T(128)} %slot_ref.3, bf16[4,1024]{1,0:T(4,128)(2,1)} %query_ref.1, bf16[4,2,128]{2,1,0:T(2,128)(2,1)} %fresh_ref.1), custom_call_target="tpu_custom_call" | custom-call | tf_op jit(solution)/shard_map/offer/pallas_call | solution.py:194
  2.0 11.9 %all-to-all-start = ((bf16[32,16,128]{2,1,0:T(8,128)(2,1)}), bf16[32,16,128]{2,1,0:T(8,128)(2,1)S(1)}, u32[]{:S(2)}, u32[]{:S(2)}) async-start(bf16[32,16,128]{2,1,0:T(8,128)(2,1)} %offer.1), calls=%async_computation | async-start | bytes 262144 | tf_op jit(solution)/shard_map/all_to_all | solution.py:201
  13.9 4.3 %stay.1 = (f32[8,8,128]{2,1,0:T(8,128)S(1)}, bf16[2048,128]{1,0:T(8,128)(2,1)S(1)}, f32[2,128]{1,0:T(2,128)S(1)}, s32[4]{0:T(128)}) custom-call(s32[1]{0:T(128)} %bitcast.own_ref, s32[128]{0:T(128)} %len_ref.1, s32[4]{0:T(128)} %slot_ref.3, s32[8,5]{1,0:T(8,128)} %moves_ref.1, bf16[4,1024]{1,0:T(4,128)(2,1)} %query_first_ref.1, bf16[4,1024]{1,0:T(4,128)(2,1)} %query_ref.1, ...), custom_call_target="tpu_custom_call" | custom-call | tf_op jit(solution)/shard_map/stay/pallas_call | solution.py:202
  18.2 5.1 %all-to-all-done.offers_ref = bf16[32,16,128]{2,1,0:T(8,128)(2,1)S(1)} async-done(((bf16[32,16,128]{2,1,0:T(8,128)(2,1)}), bf16[32,16,128]{2,1,0:T(8,128)(2,1)S(1)}, u32[]{:S(2)}, u32[]{:S(2)}) %all-to-all-start) | async-done | bytes 131104 | tf_op jit(solution)/shard_map/all_to_all | solution.py:201
  23.2 0.0 copy-start
  23.2 0.7 %copy-done = s32[4]{0:T(128)S(1)} copy-done((s32[4]{0:T(128)S(1)}, s32[4]{0:T(128)}, u32[]{:S(2)}) %copy-start) | copy-done | bytes 40
  23.9 1.2 %leave.1 = bf16[32,8,128]{2,1,0:T(8,128)(2,1)S(1)} custom-call(s32[4]{0:T(128)S(1)} %copy-done, bf16[32,16,128]{2,1,0:T(8,128)(2,1)S(1)} %all-to-all-done.offers_ref, bf16[2048,128]{1,0:T(8,128)(2,1)S(1)} %get-tuple-element.8.kept_ref, f32[2,128]{1,0:T(2,128)S(1)} %get-tuple-element.9.pair_ref), custom_call_target="tpu_custom_call" | custom-call | tf_op jit(solution)/shard_map/leave/pallas_call | solution.py:226
  25.1 12.8 %all_to_all.15.arrived_ref = bf16[32,8,128]{2,1,0:T(8,128)(2,1)S(1)} all-to-all(bf16[32,8,128]{2,1,0:T(8,128)(2,1)S(1)} %leave.1), channel_id=1, replica_groups=mesh['grp'=32,'tp'=8] {'grp'}, dimensions={0} | all-to-all | bytes 131072 | tf_op jit(solution)/shard_map/all_to_all | solution.py:234
  37.9 0.6 merge.1
  38.4 4.6 %fusion = f32[8,4096]{1,0:T(8,128)S(1)} fusion(bf16[8,1024]{1,0:T(8,128)(2,1)S(1)} %merge.1, bf16[1024,4096]{1,0:T(8,128)(2,1)} %param.16), kind=kOutput, calls=%fused_computation | convolution fusion | flops 67108864 | bytes 8536064 | tf_op jit(solution)/shard_map/dot_general | solution.py:243
  43.0 12.2 %all_to_all.16.parts_ref = f32[8,8,512]{2,1,0:T(8,128)S(1)} all-to-all(f32[8,8,512]{2,1,0:T(8,128)S(1)} %bitcast.9), channel_id=1, replica_groups=mesh['grp'=32,'tp'=8] {'tp'}, dimensions={0} | all-to-all | bytes 262144 | tf_op jit(solution)/shard_map/all_to_all | solution.py:245
  55.2 0.6 %sum.1 = (bf16[4,512]{1,0:T(4,128)(2,1)}, bf16[4,512]{1,0:T(4,128)(2,1)}) custom-call(f32[8,8,512]{2,1,0:T(8,128)S(1)} %all_to_all.16.parts_ref), custom_call_target="tpu_custom_call" | custom-call | tf_op jit(solution)/shard_map/sum/pallas_call | solution.py:247
Async XLA Ops:
  2.0 21.2 %all-to-all-start = ((bf16[32,16,128]{2,1,0:T(8,128)(2,1)}), bf16[32,16,128]{2,1,0:T(8,128)(2,1)S(1)}, u32[]{:S(2)}, u32[]{:S(2)}) async-start(bf16[32,16,128]{2,1,0:T(8,128)(2,1)} %offer.1), calls=%async_computation | async-start | bytes 262144 | tf_op jit(solution)/shard_map/all_to_all | solution.py:201
  23.2 0.7 %copy-start = (s32[4]{0:T(128)S(1)}, s32[4]{0:T(128)}, u32[]{:S(2)}) copy-start(s32[4]{0:T(128)} %get-tuple-element.6.facts_ref) | copy-start | bytes 52

commit v3 on v2

--- a/solution.py
+++ b/solution.py
@@ -14,6 +14,7 @@
 F32 = jnp.float32
 SMEM = pl.BlockSpec(memory_space=pltpu.SMEM)
 VMEM = pl.BlockSpec(memory_space=pltpu.VMEM)
+ANY = pl.BlockSpec(memory_space=pl.ANY)
 
 
 SMALL = pltpu.CompilerParams(vmem_limit_bytes=8 << 20)
@@ -40,9 +41,50 @@
     return hit_any, values
 
 
-def offer_kernel(slot_ref, query_ref, fresh_ref, out_ref):
+def fact(facts_ref, k):
+    lane = lax.broadcasted_iota(jnp.int32, facts_ref.shape, 1)
+    return jnp.sum(jnp.where(lane == k, facts_ref[...], 0.0)).astype(jnp.int32)
+
+
+def offer_kernel(
+    own_ref,
+    len_ref,
+    slot_ref,
+    moves_ref,
+    query_ref,
+    fresh_ref,
+    prompt_ref,
+    suffix_ref,
+    out_ref,
+    near_prompt_ref,
+    near_suffix_ref,
+    facts_ref,
+    sems,
+):
+    copies = (
+        pltpu.make_async_copy(prompt_ref, near_prompt_ref, sems.at[0]),
+        pltpu.make_async_copy(suffix_ref, near_suffix_ref, sems.at[1]),
+    )
+    for copy in copies:
+        copy.start()
+    own = own_ref[0]
+    slots = query_ref.shape[0]
     empty = empty_slot_of(slot_ref)
-    slots = query_ref.shape[0]
+    is_source, (out_slot, destination) = look_up(moves_ref, own, 0, (1, 2))
+    is_target, (in_source,) = look_up(moves_ref, own, 2, (0,))
+    facts = (
+        destination,
+        2 * len_ref[own * slots + out_slot],
+        out_slot,
+        jnp.maximum(slot_ref[out_slot], 0),
+        in_source,
+        jnp.where(is_target == 1, slots + empty, -1),
+    )
+    lane = lax.broadcasted_iota(jnp.int32, facts_ref.shape, 1)
+    held = jnp.zeros(facts_ref.shape, jnp.int32)
+    for k, value in enumerate(facts):
+        held = jnp.where(lane == k, value, held)
+    facts_ref[...] = held.astype(F32)
     mine = lax.broadcasted_iota(jnp.int32, (slots, HD), 0) == empty
     rows = []
     for h in range(HEADS):
@@ -54,6 +96,8 @@
     rows += [pair, jnp.zeros((6, HD), F32)]
     block = jnp.concatenate(rows, axis=0).astype(BF)
     out_ref[...] = jnp.broadcast_to(block[None], out_ref.shape)
+    for copy in copies:
+        copy.wait()
 
 
 def attend(queries, cached, pairs):
@@ -109,25 +153,15 @@
     prompt_ref,
     suffix_ref,
     rows_ref,
-    kept_ref,
     pair_ref,
-    facts_ref,
     queries_ref,
 ):
     own = own_ref[0]
     slots = query_first_ref.shape[0]
-    is_source, (out_slot, destination) = look_up(moves_ref, own, 0, (1, 2))
-    is_target, (in_source,) = look_up(moves_ref, own, 2, (0,))
-    facts_ref[0] = destination
-    facts_ref[1] = 2 * len_ref[own * slots + out_slot]
-    facts_ref[2] = in_source
-    facts_ref[3] = jnp.where(is_target == 1, slots + empty_slot_of(slot_ref), -1)
+    is_source, (out_slot,) = look_up(moves_ref, own, 0, (1,))
     for h in range(HEADS):
         queries_ref[:, h, :] = query_first_ref[:, h * HD : (h + 1) * HD].astype(F32)
         queries_ref[:, HEADS + h, :] = query_second_ref[:, h * HD : (h + 1) * HD].astype(F32)
-    half = prompt_ref.shape[1]
-    kept_ref[:half] = prompt_ref[jnp.maximum(slot_ref[out_slot], 0)]
-    kept_ref[half:] = suffix_ref[out_slot]
     pair_ref[...] = fresh_first_ref[out_slot].astype(F32)
     for s in range(slots):
         prompt_id = slot_ref[s]
@@ -145,20 +179,22 @@
         rows_ref[:, slots + s, :] = jnp.where(stays, mixed[HEADS:], 0.0)
 
 
-def leave_kernel(facts_ref, offers_ref, kept_ref, pair_ref, moved_ref):
-    offer = offers_ref[facts_ref[0]].astype(F32)
-    half = kept_ref.shape[0] // 2
+def leave_kernel(facts_ref, offers_ref, prompt_ref, suffix_ref, pair_ref, moved_ref):
+    offer = offers_ref[fact(facts_ref, 0)].astype(F32)
     mixed = attend(
         offer[:HEADS],
-        ((kept_ref[:half], None), (kept_ref[half:], facts_ref[1])),
+        (
+            (prompt_ref[fact(facts_ref, 3)], None),
+            (suffix_ref[fact(facts_ref, 2)], fact(facts_ref, 1)),
+        ),
         ((pair_ref[...], 0), (offer[HEADS : HEADS + 2], 0)),
     )
     moved_ref[...] = jnp.broadcast_to(mixed[None], moved_ref.shape)
 
 
 def merge_kernel(facts_ref, rows_ref, arrived_ref, out_ref):
-    arrived = arrived_ref[facts_ref[2]].astype(F32)
-    into = lax.broadcasted_iota(jnp.int32, rows_ref.shape[1:], 0) == facts_ref[3]
+    arrived = arrived_ref[fact(facts_ref, 4)].astype(F32)
+    into = lax.broadcasted_iota(jnp.int32, rows_ref.shape[1:], 0) == fact(facts_ref, 5)
     for h in range(HEADS):
         row = jnp.where(into, arrived[h : h + 1], rows_ref[h])
         out_ref[:, h * HD : (h + 1) * HD] = row.astype(BF)
@@ -191,24 +227,34 @@
     own = lax.axis_index("grp").astype(jnp.int32).reshape(1)
     suffix_rows = suffix_cache.reshape(slots, 2 * cap, HD)
     prompt_rows = prompt_cache.reshape(prompts, 2 * prompt_len, HD)
-    offer = pl.pallas_call(
+    offer, near_prompt, near_suffix, facts = pl.pallas_call(
         offer_kernel,
-        out_shape=pltpu.VMEM((groups, 2 * HEADS, HD), BF),
-        in_specs=[SMEM, VMEM, VMEM],
-        out_specs=VMEM,
+        out_shape=(
+            pltpu.VMEM((groups, 2 * HEADS, HD), BF),
+            pltpu.VMEM(prompt_rows.shape, BF),
+            pltpu.VMEM(suffix_rows.shape, BF),
+            pltpu.VMEM((1, HD), F32),
+        ),
+        in_specs=[SMEM] * 4 + [VMEM] * 2 + [ANY] * 2,
+        out_specs=(VMEM,) * 4,
+        scratch_shapes=[pltpu.SemaphoreType.DMA((2,))],
         name="offer",
-    )(prompt_slot, query_second, fresh_second)
+    )(
+        own,
+        suffix_len,
+        prompt_slot,
+        moves,
+        query_second,
+        fresh_second,
+        prompt_rows,
+        suffix_rows,
+    )
     offers = lax.all_to_all(offer, "grp", 0, 0, tiled=True)
-    rows, kept, pair, facts = pl.pallas_call(
+    rows, pair = pl.pallas_call(
         stay_kernel,
-        out_shape=(
-            pltpu.VMEM((HEADS, 2 * slots, HD), F32),
-            pltpu.VMEM((2 * cap + 2 * prompt_len, HD), BF),
-            pltpu.VMEM((2, HD), F32),
-            jax.ShapeDtypeStruct((4,), jnp.int32),
-        ),
+        out_shape=(pltpu.VMEM((HEADS, 2 * slots, HD), F32), pltpu.VMEM((2, HD), F32)),
         in_specs=[SMEM] * 4 + [VMEM] * 6,
-        out_specs=(VMEM, VMEM, VMEM, SMEM),
+        out_specs=(VMEM, VMEM),
         scratch_shapes=[pltpu.VMEM((slots, 2 * HEADS, HD), F32)],
         name="stay",
     )(
@@ -220,26 +266,27 @@
         query_second,
         fresh_first,
         fresh_second,
-        prompt_rows,
-        suffix_rows,
+        near(near_prompt),
+        near(near_suffix),
     )
     moved = pl.pallas_call(
         leave_kernel,
         out_shape=pltpu.VMEM((groups, HEADS, HD), BF),
-        in_specs=[SMEM, VMEM, VMEM, VMEM],
+        in_specs=[VMEM] * 5,
         out_specs=VMEM,
         compiler_params=SMALL,
+        cost_estimate=pl.CostEstimate(flops=10**11, transcendentals=0, bytes_accessed=1 << 20),
         name="leave",
-    )(facts, near(offers), near(kept), near(pair))
+    )(near(facts), near(offers), near(near_prompt), near(near_suffix), near(pair))
     arrived = lax.all_to_all(moved, "grp", 0, 0, tiled=True)
     merged = pl.pallas_call(
         merge_kernel,
         out_shape=pltpu.VMEM((2 * slots, HEADS * HD), BF),
-        in_specs=[SMEM, VMEM, VMEM],
+        in_specs=[VMEM] * 3,
         out_specs=VMEM,
         compiler_params=SMALL,
         name="merge",
-    )(facts, near(rows), near(arrived))
+    )(near(facts), near(rows), near(arrived))
     parts = jnp.dot(merged, out_weight, preferred_element_type=F32)
     parts = parts.reshape(2 * slots, shares, features // shares).swapaxes(0, 1)
     parts = lax.all_to_all(parts, "tp", 0, 0, tiled=True)

time: 56.2 us -> 52.9 us (0.941)
  matrix products: 4.58 us -> 1.19 us
  waiting for transfers between devices: 5.06 us -> 6.03 us
  local copies, waits for them, and re-layouts: 0.66 us -> 0.01 us
    dot_general x1, matrix products: 4.58 us -> 1.19 us  [per_device(): parts = jnp.dot(merged, out_weight, preferred_element_type=F32)]
    pallas_call x1, Pallas kernels: 1.38 us -> 2.8 us  [per_device(): pl.pallas_call(offer_kernel, out_shape=(pltpu.VMEM((groups, 2 * HEADS, HD...]
    all_to_all x1, waiting for transfers between devices: 5.06 us -> 6.03 us  [per_device(): offers = lax.all_to_all(offer, 'grp', 0, 0, tiled=True)]
    pallas_call x1, Pallas kernels: 4.27 us -> 3.3 us  [per_device(): pl.pallas_call(stay_kernel, out_shape=(pltpu.VMEM((HEADS, 2 * slots, HD),...]
    unnamed x2, local copies, waits for them, and re-layouts: 0.66 us -> 0.01 us
  transfers between devices with their start and end apart: 1 -> 1, of which waited for: 1 -> 1; matrix products, arithmetic and copies ran while one was open for 0% -> 0% of each run, Pallas kernels for 8% -> 6%
where the time goes in v3:
time: 52.9 us; the launch traced here: 52.5 us
  blocking collectives  25.1 us (47%)
  starting transfers between devices  11.9 us (22%)
  Pallas kernels  7.65 us (14%)
  waiting for transfers between devices  6.03 us (11%)
  matrix products  1.19 us (2%)
  between operations  0.68 us (1%)
    all_to_all x1, blocking collectives, per_device(): parts = lax.all_to_all(parts, 'tp', 0, 0, tiled=True)  12.7 us
    all_to_all x1, blocking collectives, per_device(): arrived = lax.all_to_all(moved, 'grp', 0, 0, tiled=True)  12.4 us
    all_to_all x1, starting transfers between devices, per_device(): offers = lax.all_to_all(offer, 'grp', 0, 0, tiled=True)  11.9 us
    all_to_all x1, waiting for transfers between devices, per_device(): offers = lax.all_to_all(offer, 'grp', 0, 0, tiled=True)  6.03 us
    pallas_call x1, Pallas kernels, per_device(): pl.pallas_call(stay_kernel, out_shape=(pltpu.VMEM((HEADS, 2 * slots, HD),...  3.3 us
    pallas_call x1, Pallas kernels, per_device(): pl.pallas_call(offer_kernel, out_shape=(pltpu.VMEM((groups, 2 * HEADS, HD...  2.8 us
    dot_general x1, matrix products, per_device(): parts = jnp.dot(merged, out_weight, preferred_element_type=F32)  1.19 us
  transfers between devices with their start and end apart: 1, of which 1 were waited for; matrix products, arithmetic and copies ran while one was open for 0% of the time, Pallas kernels for 6%

profile of v3, /device:TPU:1, one launch (start us, length us, event | category | flops | bytes accessed | tf_op | source)
XLA Modules:
  0.0 52.5 jit_solution(9538563594323124044)
XLA Ops:
  0.6 2.8 %offer.1 = (bf16[32,16,128]{2,1,0:T(8,128)(2,1)}, bf16[2,1024,128]{2,1,0:T(8,128)(2,1)S(1)}, bf16[4,1024,128]{2,1,0:T(8,128)(2,1)S(1)}, f32[1,128]{1,0:T(1,128)S(1)}) custom-call(s32[1]{0:T(128)} %bitcast.own_ref, s32[128]{0:T(128)} %len_ref.3, s32[4]{0:T(128)} %slot_ref.3, s32[8,5]{1,0:T(8,128)} %moves_ref.3, bf16[4,1024]{1,0:T(4,128)(2,1)} %query_second_ref.1, ...), custom_call_target="tpu_custom_call" | custom-call | tf_op jit(solution)/shard_map/offer/pallas_call | solution.py:230
  3.4 11.9 %all-to-all-start = ((bf16[32,16,128]{2,1,0:T(8,128)(2,1)}), bf16[32,16,128]{2,1,0:T(8,128)(2,1)S(1)}, u32[]{:S(2)}, u32[]{:S(2)}) async-start(bf16[32,16,128]{2,1,0:T(8,128)(2,1)} %get-tuple-element.12), calls=%async_computation | async-start | bytes 262144 | tf_op jit(solution)/shard_map/all_to_all | solution.py:252
  15.3 3.3 %stay.1 = (f32[8,8,128]{2,1,0:T(8,128)S(1)}, f32[2,128]{1,0:T(2,128)S(1)}) custom-call(s32[1]{0:T(128)} %bitcast.own_ref, s32[128]{0:T(128)} %len_ref.3, s32[4]{0:T(128)} %slot_ref.3, s32[8,5]{1,0:T(8,128)} %moves_ref.3, bf16[4,1024]{1,0:T(4,128)(2,1)} %query_first_ref.1, bf16[4,1024]{1,0:T(4,128)(2,1)} %query_second_ref.1, ...), custom_call_target="tpu_custom_call" | custom-call | tf_op jit(solution)/shard_map/stay/pallas_call | solution.py:253
  18.6 6.0 %all-to-all-done.offers_ref = bf16[32,16,128]{2,1,0:T(8,128)(2,1)S(1)} async-done(((bf16[32,16,128]{2,1,0:T(8,128)(2,1)}), bf16[32,16,128]{2,1,0:T(8,128)(2,1)S(1)}, u32[]{:S(2)}, u32[]{:S(2)}) %all-to-all-start) | async-done | bytes 131104 | tf_op jit(solution)/shard_map/all_to_all | solution.py:252
  24.7 0.0 copy-start
  24.7 0.8 %leave.1 = bf16[32,8,128]{2,1,0:T(8,128)(2,1)S(1)} custom-call(f32[1,128]{1,0:T(1,128)S(1)} %get-tuple-element.8.facts_ref, bf16[32,16,128]{2,1,0:T(8,128)(2,1)S(1)} %all-to-all-done.offers_ref, bf16[2,1024,128]{2,1,0:T(8,128)(2,1)S(1)} %get-tuple-element.9.prompt_ref, bf16[4,1024,128]{2,1,0:T(8,128)(2,1)S(1)} %get-tuple-element.10.suffix_ref, ...), custom_call_target="tpu_custom_call" | custom-call | flops 99999997952 | bytes 1048576 | tf_op jit(solution)/shard_map/leave/pallas_call | solution.py:272
  25.5 12.4 %all_to_all.15.arrived_ref = bf16[32,8,128]{2,1,0:T(8,128)(2,1)S(1)} all-to-all(bf16[32,8,128]{2,1,0:T(8,128)(2,1)S(1)} %leave.1), channel_id=1, replica_groups=mesh['grp'=32,'tp'=8] {'grp'}, dimensions={0} | all-to-all | bytes 131072 | tf_op jit(solution)/shard_map/all_to_all | solution.py:281
  37.9 0.1 merge.1
  38.0 0.0 copy-done
  38.0 1.2 %fusion = f32[8,4096]{1,0:T(8,128)S(1)} fusion(bf16[8,1024]{1,0:T(8,128)(2,1)S(1)} %merge.1, bf16[1024,4096]{1,0:T(8,128)(2,1)S(1)} %copy-done), kind=kOutput, calls=%fused_computation | convolution fusion | flops 67108864 | bytes 8536064 | tf_op jit(solution)/shard_map/dot_general | solution.py:290
  39.2 12.7 %all_to_all.16.parts_ref = f32[8,8,512]{2,1,0:T(8,128)S(1)} all-to-all(f32[8,8,512]{2,1,0:T(8,128)S(1)} %bitcast.9), channel_id=1, replica_groups=mesh['grp'=32,'tp'=8] {'tp'}, dimensions={0} | all-to-all | bytes 262144 | tf_op jit(solution)/shard_map/all_to_all | solution.py:292
  51.9 0.6 %sum.1 = (bf16[4,512]{1,0:T(4,128)(2,1)}, bf16[4,512]{1,0:T(4,128)(2,1)}) custom-call(f32[8,8,512]{2,1,0:T(8,128)S(1)} %all_to_all.16.parts_ref), custom_call_target="tpu_custom_call" | custom-call | tf_op jit(solution)/shard_map/sum/pallas_call | solution.py:294
Async XLA Ops:
  3.4 21.2 %all-to-all-start = ((bf16[32,16,128]{2,1,0:T(8,128)(2,1)}), bf16[32,16,128]{2,1,0:T(8,128)(2,1)S(1)}, u32[]{:S(2)}, u32[]{:S(2)}) async-start(bf16[32,16,128]{2,1,0:T(8,128)(2,1)} %get-tuple-element.12), calls=%async_computation | async-start | bytes 262144 | tf_op jit(solution)/shard_map/all_to_all | solution.py:252
  24.7 13.3 %copy-start = (bf16[1024,4096]{1,0:T(8,128)(2,1)S(1)}, bf16[1024,4096]{1,0:T(8,128)(2,1)}, u32[]{:S(2)}) copy-start(bf16[1024,4096]{1,0:T(8,128)(2,1)} %param.16) | copy-start | bytes 25165828

commit v4 on v2

--- a/solution.py
+++ b/solution.py
@@ -14,6 +14,7 @@
 F32 = jnp.float32
 SMEM = pl.BlockSpec(memory_space=pltpu.SMEM)
 VMEM = pl.BlockSpec(memory_space=pltpu.VMEM)
+ANY = pl.BlockSpec(memory_space=pl.ANY)
 
 
 SMALL = pltpu.CompilerParams(vmem_limit_bytes=8 << 20)
@@ -38,6 +39,11 @@
         hit_any = jnp.where(hit, jnp.int32(1), hit_any)
         values = [jnp.where(hit, moves_ref[i, f], v) for f, v in zip(fields, values)]
     return hit_any, values
+
+
+def fact(facts_ref, k):
+    lane = lax.broadcasted_iota(jnp.int32, facts_ref.shape, 1)
+    return jnp.sum(jnp.where(lane == k, facts_ref[...], 0.0)).astype(jnp.int32)
 
 
 def offer_kernel(slot_ref, query_ref, fresh_ref, out_ref):
@@ -106,29 +112,48 @@
     query_second_ref,
     fresh_first_ref,
     fresh_second_ref,
+    far_prompt_ref,
+    far_suffix_ref,
+    rows_ref,
+    pair_ref,
     prompt_ref,
     suffix_ref,
-    rows_ref,
-    kept_ref,
-    pair_ref,
     facts_ref,
     queries_ref,
+    sems,
 ):
     own = own_ref[0]
     slots = query_first_ref.shape[0]
+    prompt_copy = pltpu.make_async_copy(far_prompt_ref, prompt_ref, sems.at[slots])
+    suffix_copies = [
+        pltpu.make_async_copy(far_suffix_ref.at[s], suffix_ref.at[s], sems.at[s])
+        for s in range(slots)
+    ]
+    prompt_copy.start()
+    for copy in suffix_copies:
+        copy.start()
     is_source, (out_slot, destination) = look_up(moves_ref, own, 0, (1, 2))
     is_target, (in_source,) = look_up(moves_ref, own, 2, (0,))
-    facts_ref[0] = destination
-    facts_ref[1] = 2 * len_ref[own * slots + out_slot]
-    facts_ref[2] = in_source
-    facts_ref[3] = jnp.where(is_target == 1, slots + empty_slot_of(slot_ref), -1)
+    facts = (
+        destination,
+        2 * len_ref[own * slots + out_slot],
+        out_slot,
+        jnp.maximum(slot_ref[out_slot], 0),
+        in_source,
+        jnp.where(is_target == 1, slots + empty_slot_of(slot_ref), -1),
+    )
+    lane = lax.broadcasted_iota(jnp.int32, facts_ref.shape, 1)
+    held = jnp.zeros(facts_ref.shape, jnp.int32)
+    for k, value in enumerate(facts):
+        held = jnp.where(lane == k, value, held)
+    facts_ref[...] = held.astype(F32)
     for h in range(HEADS):
         queries_ref[:, h, :] = query_first_ref[:, h * HD : (h + 1) * HD].astype(F32)
         queries_ref[:, HEADS + h, :] = query_second_ref[:, h * HD : (h + 1) * HD].astype(F32)
-    half = prompt_ref.shape[1]
-    kept_ref[:half] = prompt_ref[jnp.maximum(slot_ref[out_slot], 0)]
-    kept_ref[half:] = suffix_ref[out_slot]
     pair_ref[...] = fresh_first_ref[out_slot].astype(F32)
+    prompt_copy.wait()
+    for copy in suffix_copies:
+        copy.wait()
     for s in range(slots):
         prompt_id = slot_ref[s]
         live = prompt_id >= 0
@@ -145,20 +170,22 @@
         rows_ref[:, slots + s, :] = jnp.where(stays, mixed[HEADS:], 0.0)
 
 
-def leave_kernel(facts_ref, offers_ref, kept_ref, pair_ref, moved_ref):
-    offer = offers_ref[facts_ref[0]].astype(F32)
-    half = kept_ref.shape[0] // 2
+def leave_kernel(facts_ref, offers_ref, prompt_ref, suffix_ref, pair_ref, moved_ref):
+    offer = offers_ref[fact(facts_ref, 0)].astype(F32)
     mixed = attend(
         offer[:HEADS],
-        ((kept_ref[:half], None), (kept_ref[half:], facts_ref[1])),
+        (
+            (prompt_ref[fact(facts_ref, 3)], None),
+            (suffix_ref[fact(facts_ref, 2)], fact(facts_ref, 1)),
+        ),
         ((pair_ref[...], 0), (offer[HEADS : HEADS + 2], 0)),
     )
     moved_ref[...] = jnp.broadcast_to(mixed[None], moved_ref.shape)
 
 
 def merge_kernel(facts_ref, rows_ref, arrived_ref, out_ref):
-    arrived = arrived_ref[facts_ref[2]].astype(F32)
-    into = lax.broadcasted_iota(jnp.int32, rows_ref.shape[1:], 0) == facts_ref[3]
+    arrived = arrived_ref[fact(facts_ref, 4)].astype(F32)
+    into = lax.broadcasted_iota(jnp.int32, rows_ref.shape[1:], 0) == fact(facts_ref, 5)
     for h in range(HEADS):
         row = jnp.where(into, arrived[h : h + 1], rows_ref[h])
         out_ref[:, h * HD : (h + 1) * HD] = row.astype(BF)
@@ -199,17 +226,21 @@
         name="offer",
     )(prompt_slot, query_second, fresh_second)
     offers = lax.all_to_all(offer, "grp", 0, 0, tiled=True)
-    rows, kept, pair, facts = pl.pallas_call(
+    rows, pair, near_prompt, near_suffix, facts = pl.pallas_call(
         stay_kernel,
         out_shape=(
             pltpu.VMEM((HEADS, 2 * slots, HD), F32),
-            pltpu.VMEM((2 * cap + 2 * prompt_len, HD), BF),
             pltpu.VMEM((2, HD), F32),
-            jax.ShapeDtypeStruct((4,), jnp.int32),
+            pltpu.VMEM(prompt_rows.shape, BF),
+            pltpu.VMEM(suffix_rows.shape, BF),
+            pltpu.VMEM((1, HD), F32),
         ),
-        in_specs=[SMEM] * 4 + [VMEM] * 6,
-        out_specs=(VMEM, VMEM, VMEM, SMEM),
-        scratch_shapes=[pltpu.VMEM((slots, 2 * HEADS, HD), F32)],
+        in_specs=[SMEM] * 4 + [VMEM] * 4 + [ANY] * 2,
+        out_specs=(VMEM,) * 5,
+        scratch_shapes=[
+            pltpu.VMEM((slots, 2 * HEADS, HD), F32),
+            pltpu.SemaphoreType.DMA((slots + 1,)),
+        ],
         name="stay",
     )(
         own,
@@ -226,20 +257,21 @@
     moved = pl.pallas_call(
         leave_kernel,
         out_shape=pltpu.VMEM((groups, HEADS, HD), BF),
-        in_specs=[SMEM, VMEM, VMEM, VMEM],
+        in_specs=[VMEM] * 5,
         out_specs=VMEM,
         compiler_params=SMALL,
+        cost_estimate=pl.CostEstimate(flops=10**11, transcendentals=0, bytes_accessed=1 << 20),
         name="leave",
-    )(facts, near(offers), near(kept), near(pair))
+    )(near(facts), near(offers), near(near_prompt), near(near_suffix), near(pair))
     arrived = lax.all_to_all(moved, "grp", 0, 0, tiled=True)
     merged = pl.pallas_call(
         merge_kernel,
         out_shape=pltpu.VMEM((2 * slots, HEADS * HD), BF),
-        in_specs=[SMEM, VMEM, VMEM],
+        in_specs=[VMEM] * 3,
         out_specs=VMEM,
         compiler_params=SMALL,
         name="merge",
-    )(facts, near(rows), near(arrived))
+    )(near(facts), near(rows), near(arrived))
     parts = jnp.dot(merged, out_weight, preferred_element_type=F32)
     parts = parts.reshape(2 * slots, shares, features // shares).swapaxes(0, 1)
     parts = lax.all_to_all(parts, "tp", 0, 0, tiled=True)

time: 56.2 us -> 51.9 us (0.923)
  matrix products: 4.58 us -> 1.19 us
  blocking collectives: 25 us -> 25.7 us
  local copies, waits for them, and re-layouts: 0.66 us -> 0.01 us
    dot_general x1, matrix products: 4.58 us -> 1.19 us  [per_device(): parts = jnp.dot(merged, out_weight, preferred_element_type=F32)]
    all_to_all x1, blocking collectives: 12.8 us -> 13.5 us  [per_device(): arrived = lax.all_to_all(moved, 'grp', 0, 0, tiled=True)]
    unnamed x2, local copies, waits for them, and re-layouts: 0.66 us -> 0.01 us
  transfers between devices with their start and end apart: 1 -> 1, of which waited for: 1 -> 1; matrix products, arithmetic and copies ran while one was open for 0% -> 0% of each run, Pallas kernels for 8% -> 9%
where the time goes in v4:
time: 51.9 us; the launch traced here: 51.6 us
  blocking collectives  25.7 us (50%)
  starting transfers between devices  11.9 us (23%)
  Pallas kernels  7.61 us (15%)
  waiting for transfers between devices  4.65 us (9%)
  matrix products  1.19 us (2%)
  between operations  0.67 us (1%)
    all_to_all x1, blocking collectives, per_device(): arrived = lax.all_to_all(moved, 'grp', 0, 0, tiled=True)  13.5 us
    all_to_all x1, blocking collectives, per_device(): parts = lax.all_to_all(parts, 'tp', 0, 0, tiled=True)  12.2 us
    all_to_all x1, starting transfers between devices, per_device(): offers = lax.all_to_all(offer, 'grp', 0, 0, tiled=True)  11.9 us
    pallas_call x1, Pallas kernels, per_device(): pl.pallas_call(stay_kernel, out_shape=(pltpu.VMEM((HEADS, 2 * slots, HD),...  4.68 us
    all_to_all x1, waiting for transfers between devices, per_device(): offers = lax.all_to_all(offer, 'grp', 0, 0, tiled=True)  4.65 us
    pallas_call x1, Pallas kernels, per_device(): pl.pallas_call(offer_kernel, out_shape=pltpu.VMEM((groups, 2 * HEADS, HD)...  1.38 us
    dot_general x1, matrix products, per_device(): parts = jnp.dot(merged, out_weight, preferred_element_type=F32)  1.19 us
  transfers between devices with their start and end apart: 1, of which 1 were waited for; matrix products, arithmetic and copies ran while one was open for 0% of the time, Pallas kernels for 9%

profile of v4, /device:TPU:1, one launch (start us, length us, event | category | flops | bytes accessed | tf_op | source)
XLA Modules:
  0.0 51.6 jit_solution(126877012770182988)
XLA Ops:
  0.6 1.4 %offer.1 = bf16[32,16,128]{2,1,0:T(8,128)(2,1)} custom-call(s32[4]{0:T(128)} %slot_ref.3, bf16[4,1024]{1,0:T(4,128)(2,1)} %query_ref.1, bf16[4,2,128]{2,1,0:T(2,128)(2,1)} %fresh_ref.1), custom_call_target="tpu_custom_call" | custom-call | tf_op jit(solution)/shard_map/offer/pallas_call | solution.py:221
  2.0 11.9 %all-to-all-start = ((bf16[32,16,128]{2,1,0:T(8,128)(2,1)}), bf16[32,16,128]{2,1,0:T(8,128)(2,1)S(1)}, u32[]{:S(2)}, u32[]{:S(2)}) async-start(bf16[32,16,128]{2,1,0:T(8,128)(2,1)} %offer.1), calls=%async_computation | async-start | bytes 262144 | tf_op jit(solution)/shard_map/all_to_all | solution.py:228
  13.9 4.7 %stay.1 = (f32[8,8,128]{2,1,0:T(8,128)S(1)}, f32[2,128]{1,0:T(2,128)S(1)}, bf16[2,1024,128]{2,1,0:T(8,128)(2,1)S(1)}, bf16[4,1024,128]{2,1,0:T(8,128)(2,1)S(1)}, f32[1,128]{1,0:T(1,128)S(1)}) custom-call(s32[1]{0:T(128)} %bitcast.own_ref, s32[128]{0:T(128)} %len_ref.1, s32[4]{0:T(128)} %slot_ref.3, s32[8,5]{1,0:T(8,128)} %moves_ref.1, ...), custom_call_target="tpu_custom_call" | custom-call | tf_op jit(solution)/shard_map/stay/pallas_call | solution.py:229
  18.6 4.6 %all-to-all-done.offers_ref = bf16[32,16,128]{2,1,0:T(8,128)(2,1)S(1)} async-done(((bf16[32,16,128]{2,1,0:T(8,128)(2,1)}), bf16[32,16,128]{2,1,0:T(8,128)(2,1)S(1)}, u32[]{:S(2)}, u32[]{:S(2)}) %all-to-all-start) | async-done | bytes 131104 | tf_op jit(solution)/shard_map/all_to_all | solution.py:228
  23.2 0.0 copy-start
  23.2 0.8 %leave.1 = bf16[32,8,128]{2,1,0:T(8,128)(2,1)S(1)} custom-call(f32[1,128]{1,0:T(1,128)S(1)} %get-tuple-element.7.facts_ref, bf16[32,16,128]{2,1,0:T(8,128)(2,1)S(1)} %all-to-all-done.offers_ref, bf16[2,1024,128]{2,1,0:T(8,128)(2,1)S(1)} %get-tuple-element.9.prompt_ref, bf16[4,1024,128]{2,1,0:T(8,128)(2,1)S(1)} %get-tuple-element.10.suffix_ref, ...), custom_call_target="tpu_custom_call" | custom-call | flops 99999997952 | bytes 1048576 | tf_op jit(solution)/shard_map/leave/pallas_call | solution.py:257
  24.0 13.5 %all_to_all.15.arrived_ref = bf16[32,8,128]{2,1,0:T(8,128)(2,1)S(1)} all-to-all(bf16[32,8,128]{2,1,0:T(8,128)(2,1)S(1)} %leave.1), channel_id=1, replica_groups=mesh['grp'=32,'tp'=8] {'grp'}, dimensions={0} | all-to-all | bytes 131072 | tf_op jit(solution)/shard_map/all_to_all | solution.py:266
  37.5 0.1 merge.1
  37.6 0.0 copy-done
  37.6 1.2 %fusion = f32[8,4096]{1,0:T(8,128)S(1)} fusion(bf16[8,1024]{1,0:T(8,128)(2,1)S(1)} %merge.1, bf16[1024,4096]{1,0:T(8,128)(2,1)S(1)} %copy-done), kind=kOutput, calls=%fused_computation | convolution fusion | flops 67108864 | bytes 8536064 | tf_op jit(solution)/shard_map/dot_general | solution.py:275
  38.8 12.2 %all_to_all.16.parts_ref = f32[8,8,512]{2,1,0:T(8,128)S(1)} all-to-all(f32[8,8,512]{2,1,0:T(8,128)S(1)} %bitcast.9), channel_id=1, replica_groups=mesh['grp'=32,'tp'=8] {'tp'}, dimensions={0} | all-to-all | bytes 262144 | tf_op jit(solution)/shard_map/all_to_all | solution.py:277
  51.0 0.6 %sum.1 = (bf16[4,512]{1,0:T(4,128)(2,1)}, bf16[4,512]{1,0:T(4,128)(2,1)}) custom-call(f32[8,8,512]{2,1,0:T(8,128)S(1)} %all_to_all.16.parts_ref), custom_call_target="tpu_custom_call" | custom-call | tf_op jit(solution)/shard_map/sum/pallas_call | solution.py:279
Async XLA Ops:
  2.0 21.2 %all-to-all-start = ((bf16[32,16,128]{2,1,0:T(8,128)(2,1)}), bf16[32,16,128]{2,1,0:T(8,128)(2,1)S(1)}, u32[]{:S(2)}, u32[]{:S(2)}) async-start(bf16[32,16,128]{2,1,0:T(8,128)(2,1)} %offer.1), calls=%async_computation | async-start | bytes 262144 | tf_op jit(solution)/shard_map/all_to_all | solution.py:228
  23.2 14.4 %copy-start = (bf16[1024,4096]{1,0:T(8,128)(2,1)S(1)}, bf16[1024,4096]{1,0:T(8,128)(2,1)}, u32[]{:S(2)}) copy-start(bf16[1024,4096]{1,0:T(8,128)(2,1)} %param.16) | copy-start | bytes 25165828

commit v5 on v4

--- a/solution.py
+++ b/solution.py
@@ -1,3 +1,5 @@
+import functools
+
 import jax
 import jax.numpy as jnp
 from jax import lax
@@ -62,76 +64,80 @@
     out_ref[...] = jnp.broadcast_to(block[None], out_ref.shape)
 
 
-def attend(queries, cached, pairs):
+def attend(samples, width_of_rows):
     scale = HD ** (-0.5)
-    narrow = queries.astype(BF)
-    row = lax.broadcasted_iota(jnp.int32, (queries.shape[0], 1), 0)
-    scores = []
-    for rows, width in cached:
-        score = (
-            lax.dot_general(
-                narrow, rows, (((1,), (1,)), ((), ())), preferred_element_type=F32
+    shape = (samples[0][0].shape[0], width_of_rows)
+    column = lax.broadcasted_iota(jnp.int32, shape, 1)
+    on_key = column % 2 == 0
+    limit = jnp.where(on_key, -1, column)
+    row = lax.broadcasted_iota(jnp.int32, (shape[0], 1), 0)
+    contract_last = (((1,), (1,)), ((), ()))
+    raw = []
+    for queries, prompt, suffix, _, _, waits in samples:
+        for wait in waits:
+            wait()
+        narrow = queries.astype(BF)
+        raw.append(
+            tuple(
+                lax.dot_general(narrow, rows, contract_last, preferred_element_type=F32)
+                for rows in (prompt(), suffix())
             )
-            * scale
         )
-        column = lax.broadcasted_iota(jnp.int32, score.shape, 1)
-        counts = column % 2 == 0
-        if width is not None:
-            counts = counts & (column < width)
-        scores.append(jnp.where(counts, score, -1e30))
-    singles = []
-    for pair, since in pairs:
-        score = jnp.sum(queries * pair[0:1], axis=1, keepdims=True) * scale
-        singles.append(jnp.where(row >= since, score, -1e30) if since else score)
-    highest = singles[0]
-    for score in singles[1:]:
-        highest = jnp.maximum(highest, score)
-    for score in scores:
-        highest = jnp.maximum(highest, jnp.max(score, axis=1, keepdims=True))
-    spreads = [jnp.exp(score - highest) for score in scores]
-    single_spreads = [jnp.exp(score - highest) for score in singles]
-    total = sum(single_spreads)
-    for spread in spreads:
-        total = total + jnp.sum(spread, axis=1, keepdims=True)
-    share = 1.0 / total
-    mixed = jnp.zeros(queries.shape, F32)
-    for (rows, _), spread in zip(cached, spreads):
-        weights = pltpu.roll(spread * share, 1, 1).astype(BF)
-        mixed += lax.dot(weights, rows, preferred_element_type=F32)
-    for (pair, _), spread in zip(pairs, single_spreads):
-        mixed += (spread * share).astype(BF).astype(F32) * pair[1:2]
-    return mixed.astype(BF)
-
-
-def stay_kernel(
-    own_ref,
-    len_ref,
-    slot_ref,
-    moves_ref,
-    query_first_ref,
-    query_second_ref,
-    fresh_first_ref,
-    fresh_second_ref,
-    far_prompt_ref,
-    far_suffix_ref,
-    rows_ref,
-    pair_ref,
-    prompt_ref,
-    suffix_ref,
-    facts_ref,
-    queries_ref,
-    sems,
-):
-    own = own_ref[0]
-    slots = query_first_ref.shape[0]
+    held = []
+    for (queries, _, _, width, pairs, _), (on_prompt, on_suffix) in zip(samples, raw):
+        scores = jnp.where(on_key, on_prompt, pltpu.roll(on_suffix, 1, 1)) * scale
+        scores = jnp.where(limit < width, scores, -1e30)
+        singles = []
+        for pair, since in pairs:
+            score = jnp.sum(queries * pair[0:1], axis=1, keepdims=True) * scale
+            singles.append(jnp.where(row >= since, score, -1e30) if since else score)
+        highest = jnp.max(scores, axis=1, keepdims=True)
+        for score in singles:
+            highest = jnp.maximum(highest, score)
+        spread = jnp.exp(scores - highest)
+        single_spreads = [jnp.exp(score - highest) for score in singles]
+        share = 1.0 / (jnp.sum(spread, axis=1, keepdims=True) + sum(single_spreads))
+        weights = spread * share
+        held.append(
+            (
+                jnp.where(on_key, 0.0, pltpu.roll(weights, 1, 1)).astype(BF),
+                jnp.where(on_key, 0.0, weights).astype(BF),
+                [(spread * share).astype(BF).astype(F32) for spread in single_spreads],
+            )
+        )
+    results = []
+    for (_, prompt, suffix, _, pairs, _), (prompt_weights, suffix_weights, single_weights) in zip(
+        samples, held
+    ):
+        mixed = lax.dot(prompt_weights, prompt(), preferred_element_type=F32)
+        mixed += lax.dot(suffix_weights, suffix(), preferred_element_type=F32)
+        for (pair, _), weight in zip(pairs, single_weights):
+            mixed += weight * pair[1:2]
+        results.append(mixed.astype(BF))
+    return results
+
+
+def stay_kernel(*refs):
+    far_prompt_ref, far_suffix_ref, *far_refs = refs[:9]
+    rows_ref, pair_ref, prompt_ref, suffix_ref, facts_ref = refs[9:14]
+    queries_ref, *near_refs, sems = refs[14:]
+    slots = suffix_ref.shape[0]
     prompt_copy = pltpu.make_async_copy(far_prompt_ref, prompt_ref, sems.at[slots])
     suffix_copies = [
         pltpu.make_async_copy(far_suffix_ref.at[s], suffix_ref.at[s], sems.at[s])
         for s in range(slots)
     ]
-    prompt_copy.start()
-    for copy in suffix_copies:
+    small_copies = [
+        pltpu.make_async_copy(far, close, sems.at[slots + 1 + k])
+        for k, (far, close) in enumerate(zip(far_refs, near_refs))
+    ]
+    for copy in (*small_copies, prompt_copy, *suffix_copies):
         copy.start()
+    own = lax.axis_index("grp")
+    for copy in small_copies:
+        copy.wait()
+    len_ref, slot_ref, moves_ref = near_refs[:3]
+    query_first_ref, query_second_ref, fresh_first_ref, fresh_second_ref = near_refs[3:]
     is_source, (out_slot, destination) = look_up(moves_ref, own, 0, (1, 2))
     is_target, (in_source,) = look_up(moves_ref, own, 2, (0,))
     facts = (
@@ -151,34 +157,42 @@
         queries_ref[:, h, :] = query_first_ref[:, h * HD : (h + 1) * HD].astype(F32)
         queries_ref[:, HEADS + h, :] = query_second_ref[:, h * HD : (h + 1) * HD].astype(F32)
     pair_ref[...] = fresh_first_ref[out_slot].astype(F32)
-    prompt_copy.wait()
-    for copy in suffix_copies:
-        copy.wait()
+    mixed = attend(
+        [
+            (
+                queries_ref[s],
+                functools.partial(prompt_ref.__getitem__, jnp.maximum(slot_ref[s], 0)),
+                functools.partial(suffix_ref.__getitem__, s),
+                2 * len_ref[own * slots + s],
+                ((fresh_first_ref[s].astype(F32), 0), (fresh_second_ref[s].astype(F32), HEADS)),
+                [suffix_copies[s].wait] if s else [prompt_copy.wait, suffix_copies[0].wait],
+            )
+            for s in range(slots)
+        ],
+        suffix_ref.shape[1],
+    )
     for s in range(slots):
-        prompt_id = slot_ref[s]
-        live = prompt_id >= 0
+        live = slot_ref[s] >= 0
         stays = live & jnp.logical_not((is_source == 1) & (out_slot == s))
-        mixed = attend(
-            queries_ref[s],
-            (
-                (prompt_ref[jnp.maximum(prompt_id, 0)], None),
-                (suffix_ref[s], 2 * len_ref[own * slots + s]),
-            ),
-            ((fresh_first_ref[s].astype(F32), 0), (fresh_second_ref[s].astype(F32), HEADS)),
-        ).astype(F32)
-        rows_ref[:, s, :] = jnp.where(live, mixed[:HEADS], 0.0)
-        rows_ref[:, slots + s, :] = jnp.where(stays, mixed[HEADS:], 0.0)
+        row = mixed[s].astype(F32)
+        rows_ref[:, s, :] = jnp.where(live, row[:HEADS], 0.0)
+        rows_ref[:, slots + s, :] = jnp.where(stays, row[HEADS:], 0.0)
 
 
 def leave_kernel(facts_ref, offers_ref, prompt_ref, suffix_ref, pair_ref, moved_ref):
     offer = offers_ref[fact(facts_ref, 0)].astype(F32)
-    mixed = attend(
-        offer[:HEADS],
-        (
-            (prompt_ref[fact(facts_ref, 3)], None),
-            (suffix_ref[fact(facts_ref, 2)], fact(facts_ref, 1)),
-        ),
-        ((pair_ref[...], 0), (offer[HEADS : HEADS + 2], 0)),
+    (mixed,) = attend(
+        [
+            (
+                offer[:HEADS],
+                functools.partial(prompt_ref.__getitem__, fact(facts_ref, 3)),
+                functools.partial(suffix_ref.__getitem__, fact(facts_ref, 2)),
+                fact(facts_ref, 1),
+                ((pair_ref[...], 0), (offer[HEADS : HEADS + 2], 0)),
+                [],
+            )
+        ],
+        suffix_ref.shape[1],
     )
     moved_ref[...] = jnp.broadcast_to(mixed[None], moved_ref.shape)
 
@@ -215,7 +229,6 @@
     groups = lax.axis_size("grp")
     shares = lax.axis_size("tp")
     features = out_weight.shape[1]
-    own = lax.axis_index("grp").astype(jnp.int32).reshape(1)
     suffix_rows = suffix_cache.reshape(slots, 2 * cap, HD)
     prompt_rows = prompt_cache.reshape(prompts, 2 * prompt_len, HD)
     offer = pl.pallas_call(
@@ -226,6 +239,8 @@
         name="offer",
     )(prompt_slot, query_second, fresh_second)
     offers = lax.all_to_all(offer, "grp", 0, 0, tiled=True)
+    tables = (suffix_len, prompt_slot, moves)
+    vectors = (query_first, query_second, fresh_first, fresh_second)
     rows, pair, near_prompt, near_suffix, facts = pl.pallas_call(
         stay_kernel,
         out_shape=(
@@ -235,25 +250,16 @@
             pltpu.VMEM(suffix_rows.shape, BF),
             pltpu.VMEM((1, HD), F32),
         ),
-        in_specs=[SMEM] * 4 + [VMEM] * 4 + [ANY] * 2,
+        in_specs=[ANY] * 9,
         out_specs=(VMEM,) * 5,
         scratch_shapes=[
             pltpu.VMEM((slots, 2 * HEADS, HD), F32),
-            pltpu.SemaphoreType.DMA((slots + 1,)),
+            *(pltpu.SMEM(table.shape, jnp.int32) for table in tables),
+            *(pltpu.VMEM(array.shape, BF) for array in vectors),
+            pltpu.SemaphoreType.DMA((slots + 1 + len(tables) + len(vectors),)),
         ],
         name="stay",
-    )(
-        own,
-        suffix_len,
-        prompt_slot,
-        moves,
-        query_first,
-        query_second,
-        fresh_first,
-        fresh_second,
-        prompt_rows,
-        suffix_rows,
-    )
+    )(prompt_rows, suffix_rows, *tables, *vectors)
     moved = pl.pallas_call(
         leave_kernel,
         out_shape=pltpu.VMEM((groups, HEADS, HD), BF),

time: 51.9 us -> 51.4 us (level)
  waiting for transfers between devices: 4.65 us -> 6.45 us
  Pallas kernels: 7.61 us -> 5.85 us
  blocking collectives: 25.7 us -> 25.1 us
    all_to_all x1, waiting for transfers between devices: 4.65 us -> 6.45 us  [per_device(): offers = lax.all_to_all(offer, 'grp', 0, 0, tiled=True)]
    pallas_call x1, Pallas kernels: 4.68 us -> 2.89 us  [per_device(): pl.pallas_call(stay_kernel, out_shape=(pltpu.VMEM((HEADS, 2 * slots, HD),...]
    all_to_all x1, blocking collectives: 13.5 us -> 12.4 us  [per_device(): arrived = lax.all_to_all(moved, 'grp', 0, 0, tiled=True)]
    all_to_all x1, blocking collectives: 12.2 us -> 12.7 us  [per_device(): parts = lax.all_to_all(parts, 'tp', 0, 0, tiled=True)]
  transfers between devices with their start and end apart: 1 -> 1, of which waited for: 1 -> 1; matrix products, arithmetic and copies ran while one was open for 0% -> 0% of each run, Pallas kernels for 9% -> 6%
where the time goes in v5:
time: 51.4 us; the launch traced here: 51.1 us
  blocking collectives  25.1 us (49%)
  starting transfers between devices  11.9 us (23%)
  waiting for transfers between devices  6.45 us (13%)
  Pallas kernels  5.85 us (11%)
  matrix products  1.19 us (2%)
  between operations  0.67 us (1%)
    all_to_all x1, blocking collectives, per_device(): parts = lax.all_to_all(parts, 'tp', 0, 0, tiled=True)  12.7 us
    all_to_all x1, blocking collectives, per_device(): arrived = lax.all_to_all(moved, 'grp', 0, 0, tiled=True)  12.4 us
    all_to_all x1, starting transfers between devices, per_device(): offers = lax.all_to_all(offer, 'grp', 0, 0, tiled=True)  11.9 us
    all_to_all x1, waiting for transfers between devices, per_device(): offers = lax.all_to_all(offer, 'grp', 0, 0, tiled=True)  6.45 us
    pallas_call x1, Pallas kernels, per_device(): pl.pallas_call(stay_kernel, out_shape=(pltpu.VMEM((HEADS, 2 * slots, HD),...  2.89 us
    pallas_call x1, Pallas kernels, per_device(): pl.pallas_call(offer_kernel, out_shape=pltpu.VMEM((groups, 2 * HEADS, HD)...  1.38 us
    dot_general x1, matrix products, per_device(): parts = jnp.dot(merged, out_weight, preferred_element_type=F32)  1.19 us
  transfers between devices with their start and end apart: 1, of which 1 were waited for; matrix products, arithmetic and copies ran while one was open for 0% of the time, Pallas kernels for 6%

profile of v5, /device:TPU:1, one launch (start us, length us, event | category | flops | bytes accessed | tf_op | source)
XLA Modules:
  0.0 51.1 jit_solution(5269002570151974693)
XLA Ops:
  0.6 1.4 %offer.1 = bf16[32,16,128]{2,1,0:T(8,128)(2,1)} custom-call(s32[4]{0:T(128)} %slot_ref.1, bf16[4,1024]{1,0:T(4,128)(2,1)} %query_ref.1, bf16[4,2,128]{2,1,0:T(2,128)(2,1)} %fresh_ref.1), custom_call_target="tpu_custom_call" | custom-call | tf_op jit(solution)/shard_map/offer/pallas_call | solution.py:234
  2.0 11.9 %all-to-all-start = ((bf16[32,16,128]{2,1,0:T(8,128)(2,1)}), bf16[32,16,128]{2,1,0:T(8,128)(2,1)S(1)}, u32[]{:S(2)}, u32[]{:S(2)}) async-start(bf16[32,16,128]{2,1,0:T(8,128)(2,1)} %offer.1), calls=%async_computation | async-start | bytes 262144 | tf_op jit(solution)/shard_map/all_to_all | solution.py:241
  13.9 2.9 %stay.1 = (f32[8,8,128]{2,1,0:T(8,128)S(1)}, f32[2,128]{1,0:T(2,128)S(1)}, bf16[2,1024,128]{2,1,0:T(8,128)(2,1)S(1)}, bf16[4,1024,128]{2,1,0:T(8,128)(2,1)S(1)}, f32[1,128]{1,0:T(1,128)S(1)}) custom-call(bf16[2,1024,128]{2,1,0:T(8,128)(2,1)} %bitcast.9, bf16[4,1024,128]{2,1,0:T(8,128)(2,1)} %bitcast.7, s32[128]{0:T(128)} %refs_2_.1, s32[4]{0:T(128)} %slot_ref.1, ...), custom_call_target="tpu_custom_call" | custom-call | tf_op jit(solution)/shard_map/stay/pallas_call | solution.py:244
  16.8 6.4 %all-to-all-done.offers_ref = bf16[32,16,128]{2,1,0:T(8,128)(2,1)S(1)} async-done(((bf16[32,16,128]{2,1,0:T(8,128)(2,1)}), bf16[32,16,128]{2,1,0:T(8,128)(2,1)S(1)}, u32[]{:S(2)}, u32[]{:S(2)}) %all-to-all-start) | async-done | bytes 131104 | tf_op jit(solution)/shard_map/all_to_all | solution.py:241
  23.2 0.0 copy-start
  23.2 0.8 %leave.1 = bf16[32,8,128]{2,1,0:T(8,128)(2,1)S(1)} custom-call(f32[1,128]{1,0:T(1,128)S(1)} %get-tuple-element.7.facts_ref, bf16[32,16,128]{2,1,0:T(8,128)(2,1)S(1)} %all-to-all-done.offers_ref, bf16[2,1024,128]{2,1,0:T(8,128)(2,1)S(1)} %get-tuple-element.9.prompt_ref, bf16[4,1024,128]{2,1,0:T(8,128)(2,1)S(1)} %get-tuple-element.10.suffix_ref, ...), custom_call_target="tpu_custom_call" | custom-call | flops 99999997952 | bytes 1048576 | tf_op jit(solution)/shard_map/leave/pallas_call | solution.py:263
  24.1 12.4 %all_to_all.15.arrived_ref = bf16[32,8,128]{2,1,0:T(8,128)(2,1)S(1)} all-to-all(bf16[32,8,128]{2,1,0:T(8,128)(2,1)S(1)} %leave.1), channel_id=1, replica_groups=mesh['grp'=32,'tp'=8] {'grp'}, dimensions={0} | all-to-all | bytes 131072 | tf_op jit(solution)/shard_map/all_to_all | solution.py:272
  36.5 0.1 merge.1
  36.6 0.0 copy-done
  36.6 1.2 %fusion = f32[8,4096]{1,0:T(8,128)S(1)} fusion(bf16[8,1024]{1,0:T(8,128)(2,1)S(1)} %merge.1, bf16[1024,4096]{1,0:T(8,128)(2,1)S(1)} %copy-done), kind=kOutput, calls=%fused_computation | convolution fusion | flops 67108864 | bytes 8536064 | tf_op jit(solution)/shard_map/dot_general | solution.py:281
  37.8 12.7 %all_to_all.16.parts_ref = f32[8,8,512]{2,1,0:T(8,128)S(1)} all-to-all(f32[8,8,512]{2,1,0:T(8,128)S(1)} %bitcast.8), channel_id=1, replica_groups=mesh['grp'=32,'tp'=8] {'tp'}, dimensions={0} | all-to-all | bytes 262144 | tf_op jit(solution)/shard_map/all_to_all | solution.py:283
  50.5 0.6 %sum.1 = (bf16[4,512]{1,0:T(4,128)(2,1)}, bf16[4,512]{1,0:T(4,128)(2,1)}) custom-call(f32[8,8,512]{2,1,0:T(8,128)S(1)} %all_to_all.16.parts_ref), custom_call_target="tpu_custom_call" | custom-call | tf_op jit(solution)/shard_map/sum/pallas_call | solution.py:285
Async XLA Ops:
  2.0 21.2 %all-to-all-start = ((bf16[32,16,128]{2,1,0:T(8,128)(2,1)}), bf16[32,16,128]{2,1,0:T(8,128)(2,1)S(1)}, u32[]{:S(2)}, u32[]{:S(2)}) async-start(bf16[32,16,128]{2,1,0:T(8,128)(2,1)} %offer.1), calls=%async_computation | async-start | bytes 262144 | tf_op jit(solution)/shard_map/all_to_all | solution.py:241
  23.2 13.4 %copy-start = (bf16[1024,4096]{1,0:T(8,128)(2,1)S(1)}, bf16[1024,4096]{1,0:T(8,128)(2,1)}, u32[]{:S(2)}) copy-start(bf16[1024,4096]{1,0:T(8,128)(2,1)} %param.16) | copy-start | bytes 25165828

commit v6 on v5

--- a/solution.py
+++ b/solution.py
@@ -51,15 +51,16 @@
 def offer_kernel(slot_ref, query_ref, fresh_ref, out_ref):
     empty = empty_slot_of(slot_ref)
     slots = query_ref.shape[0]
-    mine = lax.broadcasted_iota(jnp.int32, (slots, HD), 0) == empty
-    rows = []
-    for h in range(HEADS):
-        part = query_ref[:, h * HD : (h + 1) * HD].astype(F32)
-        rows.append(jnp.sum(jnp.where(mine, part, 0.0), axis=0, keepdims=True))
+    half = query_ref.shape[1] // 2
+    mine = lax.broadcasted_iota(jnp.int32, (slots, half), 0) == empty
     pair = jnp.zeros((2, HD), F32)
     for s in range(slots):
         pair = jnp.where(empty == s, fresh_ref[s].astype(F32), pair)
-    rows += [pair, jnp.zeros((6, HD), F32)]
+    rows = []
+    for r in range(2):
+        part = query_ref[:, r * half : (r + 1) * half].astype(F32)
+        heads = jnp.sum(jnp.where(mine, part, 0.0), axis=0, keepdims=True)
+        rows.append(jnp.concatenate([heads, pair[r : r + 1]], axis=1))
     block = jnp.concatenate(rows, axis=0).astype(BF)
     out_ref[...] = jnp.broadcast_to(block[None], out_ref.shape)
 
@@ -181,14 +182,22 @@
 
 def leave_kernel(facts_ref, offers_ref, prompt_ref, suffix_ref, pair_ref, moved_ref):
     offer = offers_ref[fact(facts_ref, 0)].astype(F32)
+    half = HEADS // 2
+    queries = jnp.concatenate(
+        [
+            offer[h // half : h // half + 1, h % half * HD : (h % half + 1) * HD]
+            for h in range(HEADS)
+        ],
+        axis=0,
+    )
     (mixed,) = attend(
         [
             (
-                offer[:HEADS],
+                queries,
                 functools.partial(prompt_ref.__getitem__, fact(facts_ref, 3)),
                 functools.partial(suffix_ref.__getitem__, fact(facts_ref, 2)),
                 fact(facts_ref, 1),
-                ((pair_ref[...], 0), (offer[HEADS : HEADS + 2], 0)),
+                ((pair_ref[...], 0), (offer[:, half * HD :], 0)),
                 [],
             )
         ],
@@ -233,7 +242,7 @@
     prompt_rows = prompt_cache.reshape(prompts, 2 * prompt_len, HD)
     offer = pl.pallas_call(
         offer_kernel,
-        out_shape=pltpu.VMEM((groups, 2 * HEADS, HD), BF),
+        out_shape=pltpu.VMEM((groups, 2, (HEADS // 2 + 1) * HD), BF),
         in_specs=[SMEM, VMEM, VMEM],
         out_specs=VMEM,
         name="offer",

time: 51.4 us -> 50.8 us (0.988)
  no operation moved by 1% of the time
where the time goes in v6:
time: 50.8 us; the launch traced here: 50.6 us
  blocking collectives  25 us (49%)
  starting transfers between devices  11.9 us (23%)
  waiting for transfers between devices  6.05 us (12%)
  Pallas kernels  5.83 us (11%)
  matrix products  1.19 us (2%)
  between operations  0.67 us (1%)
    all_to_all x1, blocking collectives, per_device(): parts = lax.all_to_all(parts, 'tp', 0, 0, tiled=True)  12.7 us
    all_to_all x1, blocking collectives, per_device(): arrived = lax.all_to_all(moved, 'grp', 0, 0, tiled=True)  12.3 us
    all_to_all x1, starting transfers between devices, per_device(): offers = lax.all_to_all(offer, 'grp', 0, 0, tiled=True)  11.9 us
    all_to_all x1, waiting for transfers between devices, per_device(): offers = lax.all_to_all(offer, 'grp', 0, 0, tiled=True)  6.05 us
    pallas_call x1, Pallas kernels, per_device(): pl.pallas_call(stay_kernel, out_shape=(pltpu.VMEM((HEADS, 2 * slots, HD),...  2.89 us
    pallas_call x1, Pallas kernels, per_device(): pl.pallas_call(offer_kernel, out_shape=pltpu.VMEM((groups, 2, (HEADS // 2...  1.37 us
    dot_general x1, matrix products, per_device(): parts = jnp.dot(merged, out_weight, preferred_element_type=F32)  1.19 us
  transfers between devices with their start and end apart: 1, of which 1 were waited for; matrix products, arithmetic and copies ran while one was open for 0% of the time, Pallas kernels for 6%

profile of v6, /device:TPU:1, one launch (start us, length us, event | category | flops | bytes accessed | tf_op | source)
XLA Modules:
  0.0 50.6 jit_solution(5241058989287313701)
XLA Ops:
  0.6 1.4 %offer.1 = bf16[32,2,640]{2,1,0:T(2,128)(2,1)} custom-call(s32[4]{0:T(128)} %slot_ref.1, bf16[4,1024]{1,0:T(4,128)(2,1)} %query_ref.1, bf16[4,2,128]{2,1,0:T(2,128)(2,1)} %fresh_ref.1), custom_call_target="tpu_custom_call" | custom-call | tf_op jit(solution)/shard_map/offer/pallas_call | solution.py:243
  2.0 11.9 %all-to-all-start = ((bf16[32,2,640]{2,1,0:T(2,128)(2,1)}), bf16[32,2,640]{2,1,0:T(2,128)(2,1)S(1)}, u32[]{:S(2)}, u32[]{:S(2)}) async-start(bf16[32,2,640]{2,1,0:T(2,128)(2,1)} %offer.1), calls=%async_computation | async-start | bytes 163840 | tf_op jit(solution)/shard_map/all_to_all | solution.py:250
  13.9 2.9 %stay.1 = (f32[8,8,128]{2,1,0:T(8,128)S(1)}, f32[2,128]{1,0:T(2,128)S(1)}, bf16[2,1024,128]{2,1,0:T(8,128)(2,1)S(1)}, bf16[4,1024,128]{2,1,0:T(8,128)(2,1)S(1)}, f32[1,128]{1,0:T(1,128)S(1)}) custom-call(bf16[2,1024,128]{2,1,0:T(8,128)(2,1)} %bitcast.9, bf16[4,1024,128]{2,1,0:T(8,128)(2,1)} %bitcast.7, s32[128]{0:T(128)} %refs_2_.1, s32[4]{0:T(128)} %slot_ref.1, ...), custom_call_target="tpu_custom_call" | custom-call | tf_op jit(solution)/shard_map/stay/pallas_call | solution.py:253
  16.8 6.1 %all-to-all-done.offers_ref = bf16[32,2,640]{2,1,0:T(2,128)(2,1)S(1)} async-done(((bf16[32,2,640]{2,1,0:T(2,128)(2,1)}), bf16[32,2,640]{2,1,0:T(2,128)(2,1)S(1)}, u32[]{:S(2)}, u32[]{:S(2)}) %all-to-all-start) | async-done | bytes 81952 | tf_op jit(solution)/shard_map/all_to_all | solution.py:250
  22.8 0.0 copy-start
  22.8 0.8 %leave.1 = bf16[32,8,128]{2,1,0:T(8,128)(2,1)S(1)} custom-call(f32[1,128]{1,0:T(1,128)S(1)} %get-tuple-element.7.facts_ref, bf16[32,2,640]{2,1,0:T(2,128)(2,1)S(1)} %all-to-all-done.offers_ref, bf16[2,1024,128]{2,1,0:T(8,128)(2,1)S(1)} %get-tuple-element.9.prompt_ref, bf16[4,1024,128]{2,1,0:T(8,128)(2,1)S(1)} %get-tuple-element.10.suffix_ref, ...), custom_call_target="tpu_custom_call" | custom-call | flops 99999997952 | bytes 1048576 | tf_op jit(solution)/shard_map/leave/pallas_call | solution.py:272
  23.7 12.3 %all_to_all.15.arrived_ref = bf16[32,8,128]{2,1,0:T(8,128)(2,1)S(1)} all-to-all(bf16[32,8,128]{2,1,0:T(8,128)(2,1)S(1)} %leave.1), channel_id=1, replica_groups=mesh['grp'=32,'tp'=8] {'grp'}, dimensions={0} | all-to-all | bytes 131072 | tf_op jit(solution)/shard_map/all_to_all | solution.py:281
  35.9 0.1 merge.1
  36.1 0.0 copy-done
  36.1 1.2 %fusion = f32[8,4096]{1,0:T(8,128)S(1)} fusion(bf16[8,1024]{1,0:T(8,128)(2,1)S(1)} %merge.1, bf16[1024,4096]{1,0:T(8,128)(2,1)S(1)} %copy-done), kind=kOutput, calls=%fused_computation | convolution fusion | flops 67108864 | bytes 8536064 | tf_op jit(solution)/shard_map/dot_general | solution.py:290
  37.3 12.7 %all_to_all.16.parts_ref = f32[8,8,512]{2,1,0:T(8,128)S(1)} all-to-all(f32[8,8,512]{2,1,0:T(8,128)S(1)} %bitcast.8), channel_id=1, replica_groups=mesh['grp'=32,'tp'=8] {'tp'}, dimensions={0} | all-to-all | bytes 262144 | tf_op jit(solution)/shard_map/all_to_all | solution.py:292
  50.0 0.6 %sum.1 = (bf16[4,512]{1,0:T(4,128)(2,1)}, bf16[4,512]{1,0:T(4,128)(2,1)}) custom-call(f32[8,8,512]{2,1,0:T(8,128)S(1)} %all_to_all.16.parts_ref), custom_call_target="tpu_custom_call" | custom-call | tf_op jit(solution)/shard_map/sum/pallas_call | solution.py:294
Async XLA Ops:
  2.0 20.8 %all-to-all-start = ((bf16[32,2,640]{2,1,0:T(2,128)(2,1)}), bf16[32,2,640]{2,1,0:T(2,128)(2,1)S(1)}, u32[]{:S(2)}, u32[]{:S(2)}) async-start(bf16[32,2,640]{2,1,0:T(2,128)(2,1)} %offer.1), calls=%async_computation | async-start | bytes 163840 | tf_op jit(solution)/shard_map/all_to_all | solution.py:250
  22.8 13.2 %copy-start = (bf16[1024,4096]{1,0:T(8,128)(2,1)S(1)}, bf16[1024,4096]{1,0:T(8,128)(2,1)}, u32[]{:S(2)}) copy-start(bf16[1024,4096]{1,0:T(8,128)(2,1)} %param.16) | copy-start | bytes 25165828

commit v7 on v6

--- a/solution.py
+++ b/solution.py
@@ -215,7 +215,7 @@
 
 
 def sum_kernel(parts_ref, first_ref, second_ref):
-    total = jnp.sum(parts_ref[...], axis=0)
+    total = jnp.sum(parts_ref[...].astype(F32), axis=0)
     slots = first_ref.shape[0]
     first_ref[...] = total[:slots].astype(BF)
     second_ref[...] = total[slots:].astype(BF)
@@ -287,7 +287,7 @@
         compiler_params=SMALL,
         name="merge",
     )(near(facts), near(rows), near(arrived))
-    parts = jnp.dot(merged, out_weight, preferred_element_type=F32)
+    parts = jnp.dot(merged, out_weight, preferred_element_type=F32).astype(BF)
     parts = parts.reshape(2 * slots, shares, features // shares).swapaxes(0, 1)
     parts = lax.all_to_all(parts, "tp", 0, 0, tiled=True)
     out = jax.ShapeDtypeStruct((slots, features // shares), BF)

time: 50.8 us -> 50.5 us (level)
  no operation moved by 1% of the time
where the time goes in v7:
time: 50.5 us; the launch traced here: 50.2 us
  blocking collectives  24.6 us (49%)
  starting transfers between devices  11.9 us (24%)
  waiting for transfers between devices  6.05 us (12%)
  Pallas kernels  5.84 us (12%)
  matrix products  1.19 us (2%)
  between operations  0.67 us (1%)
    all_to_all x1, blocking collectives, per_device(): parts = lax.all_to_all(parts, 'tp', 0, 0, tiled=True)  12.3 us
    all_to_all x1, blocking collectives, per_device(): arrived = lax.all_to_all(moved, 'grp', 0, 0, tiled=True)  12.3 us
    all_to_all x1, starting transfers between devices, per_device(): offers = lax.all_to_all(offer, 'grp', 0, 0, tiled=True)  11.9 us
    all_to_all x1, waiting for transfers between devices, per_device(): offers = lax.all_to_all(offer, 'grp', 0, 0, tiled=True)  6.05 us
    pallas_call x1, Pallas kernels, per_device(): pl.pallas_call(stay_kernel, out_shape=(pltpu.VMEM((HEADS, 2 * slots, HD),...  2.89 us
    pallas_call x1, Pallas kernels, per_device(): pl.pallas_call(offer_kernel, out_shape=pltpu.VMEM((groups, 2, (HEADS // 2...  1.37 us
    dot_general x1, matrix products, per_device(): parts = jnp.dot(merged, out_weight, preferred_element_type=F32).astype(BF)  1.19 us
  transfers between devices with their start and end apart: 1, of which 1 were waited for; matrix products, arithmetic and copies ran while one was open for 0% of the time, Pallas kernels for 6%

profile of v7, /device:TPU:1, one launch (start us, length us, event | category | flops | bytes accessed | tf_op | source)
XLA Modules:
  0.0 50.2 jit_solution(10960735730174173208)
XLA Ops:
  0.6 1.4 %offer.1 = bf16[32,2,640]{2,1,0:T(2,128)(2,1)} custom-call(s32[4]{0:T(128)} %slot_ref.1, bf16[4,1024]{1,0:T(4,128)(2,1)} %query_ref.1, bf16[4,2,128]{2,1,0:T(2,128)(2,1)} %fresh_ref.1), custom_call_target="tpu_custom_call" | custom-call | tf_op jit(solution)/shard_map/offer/pallas_call | solution.py:243
  2.0 11.9 %all-to-all-start = ((bf16[32,2,640]{2,1,0:T(2,128)(2,1)}), bf16[32,2,640]{2,1,0:T(2,128)(2,1)S(1)}, u32[]{:S(2)}, u32[]{:S(2)}) async-start(bf16[32,2,640]{2,1,0:T(2,128)(2,1)} %offer.1), calls=%async_computation | async-start | bytes 163840 | tf_op jit(solution)/shard_map/all_to_all | solution.py:250
  13.9 2.9 %stay.1 = (f32[8,8,128]{2,1,0:T(8,128)S(1)}, f32[2,128]{1,0:T(2,128)S(1)}, bf16[2,1024,128]{2,1,0:T(8,128)(2,1)S(1)}, bf16[4,1024,128]{2,1,0:T(8,128)(2,1)S(1)}, f32[1,128]{1,0:T(1,128)S(1)}) custom-call(bf16[2,1024,128]{2,1,0:T(8,128)(2,1)} %bitcast.8, bf16[4,1024,128]{2,1,0:T(8,128)(2,1)} %bitcast.7, s32[128]{0:T(128)} %refs_2_.1, s32[4]{0:T(128)} %slot_ref.1, ...), custom_call_target="tpu_custom_call" | custom-call | tf_op jit(solution)/shard_map/stay/pallas_call | solution.py:253
  16.8 6.1 %all-to-all-done.offers_ref = bf16[32,2,640]{2,1,0:T(2,128)(2,1)S(1)} async-done(((bf16[32,2,640]{2,1,0:T(2,128)(2,1)}), bf16[32,2,640]{2,1,0:T(2,128)(2,1)S(1)}, u32[]{:S(2)}, u32[]{:S(2)}) %all-to-all-start) | async-done | bytes 81952 | tf_op jit(solution)/shard_map/all_to_all | solution.py:250
  22.8 0.0 copy-start
  22.8 0.8 %leave.1 = bf16[32,8,128]{2,1,0:T(8,128)(2,1)S(1)} custom-call(f32[1,128]{1,0:T(1,128)S(1)} %get-tuple-element.7.facts_ref, bf16[32,2,640]{2,1,0:T(2,128)(2,1)S(1)} %all-to-all-done.offers_ref, bf16[2,1024,128]{2,1,0:T(8,128)(2,1)S(1)} %get-tuple-element.9.prompt_ref, bf16[4,1024,128]{2,1,0:T(8,128)(2,1)S(1)} %get-tuple-element.10.suffix_ref, ...), custom_call_target="tpu_custom_call" | custom-call | flops 99999997952 | bytes 1048576 | tf_op jit(solution)/shard_map/leave/pallas_call | solution.py:272
  23.7 12.3 %all_to_all.15.arrived_ref = bf16[32,8,128]{2,1,0:T(8,128)(2,1)S(1)} all-to-all(bf16[32,8,128]{2,1,0:T(8,128)(2,1)S(1)} %leave.1), channel_id=1, replica_groups=mesh['grp'=32,'tp'=8] {'grp'}, dimensions={0} | all-to-all | bytes 131072 | tf_op jit(solution)/shard_map/all_to_all | solution.py:281
  35.9 0.1 merge.1
  36.1 0.0 copy-done
  36.1 1.2 %convolution_convert_fusion = bf16[8,4096]{1,0:T(8,128)(2,1)S(1)} fusion(bf16[8,1024]{1,0:T(8,128)(2,1)S(1)} %merge.1, bf16[1024,4096]{1,0:T(8,128)(2,1)S(1)} %copy-done), kind=kOutput, calls=%fused_computation | convolution fusion | flops 67141632 | bytes 8470528 | tf_op jit(solution)/shard_map/dot_general | solution.py:290
  37.3 12.3 %all_to_all.16.parts_ref = bf16[8,8,512]{2,1,0:T(8,128)(2,1)S(1)} all-to-all(bf16[8,8,512]{2,1,0:T(8,128)(2,1)S(1)} %bitcast.9), channel_id=1, replica_groups=mesh['grp'=32,'tp'=8] {'tp'}, dimensions={0} | all-to-all | bytes 131072 | tf_op jit(solution)/shard_map/all_to_all | solution.py:292
  49.6 0.6 %sum.1 = (bf16[4,512]{1,0:T(4,128)(2,1)}, bf16[4,512]{1,0:T(4,128)(2,1)}) custom-call(bf16[8,8,512]{2,1,0:T(8,128)(2,1)S(1)} %all_to_all.16.parts_ref), custom_call_target="tpu_custom_call" | custom-call | tf_op jit(solution)/shard_map/sum/pallas_call | solution.py:294
Async XLA Ops:
  2.0 20.8 %all-to-all-start = ((bf16[32,2,640]{2,1,0:T(2,128)(2,1)}), bf16[32,2,640]{2,1,0:T(2,128)(2,1)S(1)}, u32[]{:S(2)}, u32[]{:S(2)}) async-start(bf16[32,2,640]{2,1,0:T(2,128)(2,1)} %offer.1), calls=%async_computation | async-start | bytes 163840 | tf_op jit(solution)/shard_map/all_to_all | solution.py:250
  22.8 13.2 %copy-start = (bf16[1024,4096]{1,0:T(8,128)(2,1)S(1)}, bf16[1024,4096]{1,0:T(8,128)(2,1)}, u32[]{:S(2)}) copy-start(bf16[1024,4096]{1,0:T(8,128)(2,1)} %param.16) | copy-start | bytes 25165828

commit v8 on v7

--- a/solution.py
+++ b/solution.py
@@ -120,8 +120,8 @@
 
 def stay_kernel(*refs):
     far_prompt_ref, far_suffix_ref, *far_refs = refs[:9]
-    rows_ref, pair_ref, prompt_ref, suffix_ref, facts_ref = refs[9:14]
-    queries_ref, *near_refs, sems = refs[14:]
+    rows_ref, pair_ref, kept_ref, facts_ref = refs[9:13]
+    prompt_ref, suffix_ref, queries_ref, *near_refs, sems = refs[13:]
     slots = suffix_ref.shape[0]
     prompt_copy = pltpu.make_async_copy(far_prompt_ref, prompt_ref, sems.at[slots])
     suffix_copies = [
@@ -141,11 +141,17 @@
     query_first_ref, query_second_ref, fresh_first_ref, fresh_second_ref = near_refs[3:]
     is_source, (out_slot, destination) = look_up(moves_ref, own, 0, (1, 2))
     is_target, (in_source,) = look_up(moves_ref, own, 2, (0,))
+    last = slots + 1 + len(small_copies)
+    own_prompt = far_prompt_ref.at[jnp.maximum(slot_ref[out_slot], 0)]
+    kept_copies = (
+        pltpu.make_async_copy(own_prompt, kept_ref.at[0], sems.at[last]),
+        pltpu.make_async_copy(far_suffix_ref.at[out_slot], kept_ref.at[1], sems.at[last + 1]),
+    )
+    for copy in kept_copies:
+        copy.start()
     facts = (
         destination,
         2 * len_ref[own * slots + out_slot],
-        out_slot,
-        jnp.maximum(slot_ref[out_slot], 0),
         in_source,
         jnp.where(is_target == 1, slots + empty_slot_of(slot_ref), -1),
     )
@@ -178,9 +184,11 @@
         row = mixed[s].astype(F32)
         rows_ref[:, s, :] = jnp.where(live, row[:HEADS], 0.0)
         rows_ref[:, slots + s, :] = jnp.where(stays, row[HEADS:], 0.0)
-
-
-def leave_kernel(facts_ref, offers_ref, prompt_ref, suffix_ref, pair_ref, moved_ref):
+    for copy in kept_copies:
+        copy.wait()
+
+
+def leave_kernel(facts_ref, offers_ref, kept_ref, pair_ref, moved_ref):
     offer = offers_ref[fact(facts_ref, 0)].astype(F32)
     half = HEADS // 2
     queries = jnp.concatenate(
@@ -194,21 +202,21 @@
         [
             (
                 queries,
-                functools.partial(prompt_ref.__getitem__, fact(facts_ref, 3)),
-                functools.partial(suffix_ref.__getitem__, fact(facts_ref, 2)),
+                functools.partial(kept_ref.__getitem__, 0),
+                functools.partial(kept_ref.__getitem__, 1),
                 fact(facts_ref, 1),
                 ((pair_ref[...], 0), (offer[:, half * HD :], 0)),
                 [],
             )
         ],
-        suffix_ref.shape[1],
+        kept_ref.shape[1],
     )
     moved_ref[...] = jnp.broadcast_to(mixed[None], moved_ref.shape)
 
 
 def merge_kernel(facts_ref, rows_ref, arrived_ref, out_ref):
-    arrived = arrived_ref[fact(facts_ref, 4)].astype(F32)
-    into = lax.broadcasted_iota(jnp.int32, rows_ref.shape[1:], 0) == fact(facts_ref, 5)
+    arrived = arrived_ref[fact(facts_ref, 2)].astype(F32)
+    into = lax.broadcasted_iota(jnp.int32, rows_ref.shape[1:], 0) == fact(facts_ref, 3)
     for h in range(HEADS):
         row = jnp.where(into, arrived[h : h + 1], rows_ref[h])
         out_ref[:, h * HD : (h + 1) * HD] = row.astype(BF)
@@ -250,34 +258,35 @@
     offers = lax.all_to_all(offer, "grp", 0, 0, tiled=True)
     tables = (suffix_len, prompt_slot, moves)
     vectors = (query_first, query_second, fresh_first, fresh_second)
-    rows, pair, near_prompt, near_suffix, facts = pl.pallas_call(
+    rows, pair, kept, facts = pl.pallas_call(
         stay_kernel,
         out_shape=(
             pltpu.VMEM((HEADS, 2 * slots, HD), F32),
             pltpu.VMEM((2, HD), F32),
-            pltpu.VMEM(prompt_rows.shape, BF),
-            pltpu.VMEM(suffix_rows.shape, BF),
+            pltpu.VMEM((2, *suffix_rows.shape[1:]), BF),
             pltpu.VMEM((1, HD), F32),
         ),
         in_specs=[ANY] * 9,
-        out_specs=(VMEM,) * 5,
+        out_specs=(VMEM,) * 4,
         scratch_shapes=[
+            pltpu.VMEM(prompt_rows.shape, BF),
+            pltpu.VMEM(suffix_rows.shape, BF),
             pltpu.VMEM((slots, 2 * HEADS, HD), F32),
             *(pltpu.SMEM(table.shape, jnp.int32) for table in tables),
             *(pltpu.VMEM(array.shape, BF) for array in vectors),
-            pltpu.SemaphoreType.DMA((slots + 1 + len(tables) + len(vectors),)),
+            pltpu.SemaphoreType.DMA((slots + 3 + len(tables) + len(vectors),)),
         ],
         name="stay",
     )(prompt_rows, suffix_rows, *tables, *vectors)
     moved = pl.pallas_call(
         leave_kernel,
         out_shape=pltpu.VMEM((groups, HEADS, HD), BF),
-        in_specs=[VMEM] * 5,
+        in_specs=[VMEM] * 4,
         out_specs=VMEM,
         compiler_params=SMALL,
         cost_estimate=pl.CostEstimate(flops=10**11, transcendentals=0, bytes_accessed=1 << 20),
         name="leave",
-    )(near(facts), near(offers), near(near_prompt), near(near_suffix), near(pair))
+    )(near(facts), near(offers), near(kept), near(pair))
     arrived = lax.all_to_all(moved, "grp", 0, 0, tiled=True)
     merged = pl.pallas_call(
         merge_kernel,

time: 50.5 us -> 50.4 us (level)
  no operation moved by 1% of the time
where the time goes in v8:
time: 50.4 us; the launch traced here: 50.2 us
  blocking collectives  24.6 us (49%)
  starting transfers between devices  11.9 us (24%)
  waiting for transfers between devices  6.04 us (12%)
  Pallas kernels  5.82 us (12%)
  matrix products  1.19 us (2%)
  between operations  0.67 us (1%)
    all_to_all x1, blocking collectives, per_device(): parts = lax.all_to_all(parts, 'tp', 0, 0, tiled=True)  12.3 us
    all_to_all x1, blocking collectives, per_device(): arrived = lax.all_to_all(moved, 'grp', 0, 0, tiled=True)  12.3 us
    all_to_all x1, starting transfers between devices, per_device(): offers = lax.all_to_all(offer, 'grp', 0, 0, tiled=True)  11.9 us
    all_to_all x1, waiting for transfers between devices, per_device(): offers = lax.all_to_all(offer, 'grp', 0, 0, tiled=True)  6.04 us
    pallas_call x1, Pallas kernels, per_device(): pl.pallas_call(stay_kernel, out_shape=(pltpu.VMEM((HEADS, 2 * slots, HD),...  2.91 us
    pallas_call x1, Pallas kernels, per_device(): pl.pallas_call(offer_kernel, out_shape=pltpu.VMEM((groups, 2, (HEADS // 2...  1.37 us
    dot_general x1, matrix products, per_device(): parts = jnp.dot(merged, out_weight, preferred_element_type=F32).astype(BF)  1.19 us
  transfers between devices with their start and end apart: 1, of which 1 were waited for; matrix products, arithmetic and copies ran while one was open for 0% of the time, Pallas kernels for 6%

profile of v8, /device:TPU:1, one launch (start us, length us, event | category | flops | bytes accessed | tf_op | source)
XLA Modules:
  0.0 50.2 jit_solution(18158127971206678042)
XLA Ops:
  0.6 1.4 %offer.1 = bf16[32,2,640]{2,1,0:T(2,128)(2,1)} custom-call(s32[4]{0:T(128)} %slot_ref.1, bf16[4,1024]{1,0:T(4,128)(2,1)} %query_ref.1, bf16[4,2,128]{2,1,0:T(2,128)(2,1)} %fresh_ref.1), custom_call_target="tpu_custom_call" | custom-call | tf_op jit(solution)/shard_map/offer/pallas_call | solution.py:251
  2.0 11.9 %all-to-all-start = ((bf16[32,2,640]{2,1,0:T(2,128)(2,1)}), bf16[32,2,640]{2,1,0:T(2,128)(2,1)S(1)}, u32[]{:S(2)}, u32[]{:S(2)}) async-start(bf16[32,2,640]{2,1,0:T(2,128)(2,1)} %offer.1), calls=%async_computation | async-start | bytes 163840 | tf_op jit(solution)/shard_map/all_to_all | solution.py:258
  13.9 2.9 %stay.1 = (f32[8,8,128]{2,1,0:T(8,128)S(1)}, f32[2,128]{1,0:T(2,128)S(1)}, bf16[2,1024,128]{2,1,0:T(8,128)(2,1)S(1)}, f32[1,128]{1,0:T(1,128)S(1)}) custom-call(bf16[2,1024,128]{2,1,0:T(8,128)(2,1)} %bitcast.8, bf16[4,1024,128]{2,1,0:T(8,128)(2,1)} %bitcast.7, s32[128]{0:T(128)} %refs_2_.1, s32[4]{0:T(128)} %slot_ref.1, s32[8,5]{1,0:T(8,128)} %refs_4_.1, ...), custom_call_target="tpu_custom_call" | custom-call | tf_op jit(solution)/shard_map/stay/pallas_call | solution.py:261
  16.8 6.0 %all-to-all-done.offers_ref = bf16[32,2,640]{2,1,0:T(2,128)(2,1)S(1)} async-done(((bf16[32,2,640]{2,1,0:T(2,128)(2,1)}), bf16[32,2,640]{2,1,0:T(2,128)(2,1)S(1)}, u32[]{:S(2)}, u32[]{:S(2)}) %all-to-all-start) | async-done | bytes 81952 | tf_op jit(solution)/shard_map/all_to_all | solution.py:258
  22.8 0.0 copy-start
  22.8 0.8 %leave.1 = bf16[32,8,128]{2,1,0:T(8,128)(2,1)S(1)} custom-call(f32[1,128]{1,0:T(1,128)S(1)} %get-tuple-element.6.facts_ref, bf16[32,2,640]{2,1,0:T(2,128)(2,1)S(1)} %all-to-all-done.offers_ref, bf16[2,1024,128]{2,1,0:T(8,128)(2,1)S(1)} %get-tuple-element.8.kept_ref, f32[2,128]{1,0:T(2,128)S(1)} %get-tuple-element.9.pair_ref), custom_call_target="tpu_custom_call" | custom-call | flops 99999997952 | bytes 1048576 | tf_op jit(solution)/shard_map/leave/pallas_call | solution.py:281
  23.6 12.3 %all_to_all.15.arrived_ref = bf16[32,8,128]{2,1,0:T(8,128)(2,1)S(1)} all-to-all(bf16[32,8,128]{2,1,0:T(8,128)(2,1)S(1)} %leave.1), channel_id=1, replica_groups=mesh['grp'=32,'tp'=8] {'grp'}, dimensions={0} | all-to-all | bytes 131072 | tf_op jit(solution)/shard_map/all_to_all | solution.py:290
  35.9 0.1 merge.1
  36.0 0.0 copy-done
  36.0 1.2 %convolution_convert_fusion = bf16[8,4096]{1,0:T(8,128)(2,1)S(1)} fusion(bf16[8,1024]{1,0:T(8,128)(2,1)S(1)} %merge.1, bf16[1024,4096]{1,0:T(8,128)(2,1)S(1)} %copy-done), kind=kOutput, calls=%fused_computation | convolution fusion | flops 67141632 | bytes 8470528 | tf_op jit(solution)/shard_map/dot_general | solution.py:299
  37.2 12.3 %all_to_all.16.parts_ref = bf16[8,8,512]{2,1,0:T(8,128)(2,1)S(1)} all-to-all(bf16[8,8,512]{2,1,0:T(8,128)(2,1)S(1)} %bitcast.9), channel_id=1, replica_groups=mesh['grp'=32,'tp'=8] {'tp'}, dimensions={0} | all-to-all | bytes 131072 | tf_op jit(solution)/shard_map/all_to_all | solution.py:301
  49.6 0.6 %sum.1 = (bf16[4,512]{1,0:T(4,128)(2,1)}, bf16[4,512]{1,0:T(4,128)(2,1)}) custom-call(bf16[8,8,512]{2,1,0:T(8,128)(2,1)S(1)} %all_to_all.16.parts_ref), custom_call_target="tpu_custom_call" | custom-call | tf_op jit(solution)/shard_map/sum/pallas_call | solution.py:303
Async XLA Ops:
  2.0 20.8 %all-to-all-start = ((bf16[32,2,640]{2,1,0:T(2,128)(2,1)}), bf16[32,2,640]{2,1,0:T(2,128)(2,1)S(1)}, u32[]{:S(2)}, u32[]{:S(2)}) async-start(bf16[32,2,640]{2,1,0:T(2,128)(2,1)} %offer.1), calls=%async_computation | async-start | bytes 163840 | tf_op jit(solution)/shard_map/all_to_all | solution.py:258
  22.8 13.2 %copy-start = (bf16[1024,4096]{1,0:T(8,128)(2,1)S(1)}, bf16[1024,4096]{1,0:T(8,128)(2,1)}, u32[]{:S(2)}) copy-start(bf16[1024,4096]{1,0:T(8,128)(2,1)} %param.16) | copy-start | bytes 25165828
